TPU v7x, 128 devices: a whole 4x4x4 slice. The times are simulated.
128 devices in a mesh: data: 32 (over z, y, x_hi), width: 4 (over x_lo, core).
Axes of the slice: x: 4 (x_hi: 2, x_lo: 2; x = x_hi * 2 + x_lo), y: 4, z: 4, core: 2. Of those that a mesh axis runs over, the one named last changes fastest.
Arguments:
- grad_up: float32 [32, 768, 3072], P('data', None, 'width'), may hold values from -6 to 6
- grad_down: float32 [32, 3072, 768], P('data', 'width'), may hold values from -6 to 6
- grad_query: float32 [32, 768, 768], P('data', None, 'width'), may hold values from -6 to 6
- grad_key: float32 [32, 768, 768], P('data', None, 'width'), may hold values from -6 to 6
- grad_value: float32 [32, 768, 768], P('data', None, 'width'), may hold values from -6 to 6
- grad_mixed: float32 [32, 768, 768], P('data', 'width'), may hold values from -6 to 6
- grad_norm: float32 [32, 768], P('data'), may hold values from -12 to 12
- weight_up: float32 [768, 3072], P('data', 'width'), may hold values from -0.21875 to 0.21875
- weight_down: float32 [3072, 768], P('width', 'data'), may hold values from -0.109375 to 0.109375
- weight_query: float32 [768, 768], P('data', 'width'), may hold values from -0.21875 to 0.21875
- weight_key: float32 [768, 768], P('data', 'width'), may hold values from -0.21875 to 0.21875
- weight_value: float32 [768, 768], P('data', 'width'), may hold values from -0.21875 to 0.21875
- weight_mixed: float32 [768, 768], P('width', 'data'), may hold values from -0.21875 to 0.21875
- weight_norm: float32 [768], P('data'), may hold values from 0.25 to 1.75
- moment_up: float32 [768, 3072], P('data', 'width'), may hold values from 0.05 to 0.8
- moment_down: float32 [3072, 768], P('width', 'data'), may hold values from 0.05 to 0.8
- moment_query: float32 [768, 768], P('data', 'width'), may hold values from 0.05 to 0.8
- moment_key: float32 [768, 768], P('data', 'width'), may hold values from 0.05 to 0.8
- moment_value: float32 [768, 768], P('data', 'width'), may hold values from 0.05 to 0.8
- moment_mixed: float32 [768, 768], P('width', 'data'), may hold values from 0.05 to 0.8
- moment_norm: float32 [768], P('data'), may hold values from 0.05 to 0.8
Outputs:
- copy_up: bfloat16 [768, 3072], P(None, 'width')
- copy_down: bfloat16 [3072, 768], P('width')
- copy_query: bfloat16 [768, 768], P(None, 'width')
- copy_key: bfloat16 [768, 768], P(None, 'width')
- copy_value: bfloat16 [768, 768], P(None, 'width')
- copy_mixed: bfloat16 [768, 768], P('width')
- copy_norm: bfloat16 [768], replicated
- new_up: float32 [768, 3072], P('data', 'width')
- new_down: float32 [3072, 768], P('width', 'data')
- new_query: float32 [768, 768], P('data', 'width')
- new_key: float32 [768, 768], P('data', 'width')
- new_value: float32 [768, 768], P('data', 'width')
- new_mixed: float32 [768, 768], P('width', 'data')
- new_norm: float32 [768], P('data')
- state_new_up: float32 [768, 3072], P('data', 'width')
- state_new_down: float32 [3072, 768], P('width', 'data')
- state_new_query: float32 [768, 768], P('data', 'width')
- state_new_key: float32 [768, 768], P('data', 'width')
- state_new_value: float32 [768, 768], P('data', 'width')
- state_new_mixed: float32 [768, 768], P('width', 'data')
- state_new_norm: float32 [768], P('data')
All inputs are finite; a program needn't handle non-finite values.
Results may differ from a plain program's by a relative error of at most 0.0004.
Values may be sent and summed in bfloat16 or wider, within the bound.
A program may use at most 128 MiB of HBM per device.

v0:
```python
import jax
import jax.numpy as jnp
from jax import lax
from jax.sharding import PartitionSpec as P

learn_rate = 0.05
hold_rate = 0.9


def in_blocks(x, dim, devices):
    shape = x.shape
    blocks = x.reshape(*shape[:dim], devices, shape[dim] // devices, *shape[dim + 1 :])
    return jnp.moveaxis(blocks, dim, 0)


def one_scatter(arrays, axis, dims):
    devices = lax.axis_size(axis)
    blocks = [in_blocks(a, dim, devices) for a, dim in zip(arrays, dims)]
    lines = jnp.concatenate([b.reshape(devices, -1) for b in blocks], axis=1)
    span = max(16, -(-lines.shape[1] // 1024) * 8)
    lines = jnp.pad(lines, ((0, 0), (0, span * 128 - lines.shape[1]))).reshape(-1, 128)
    line, at, gathered = (lax.psum_scatter(lines, axis, tiled=True).reshape(-1), 0, [])
    for b in blocks:
        part = b[0]
        gathered.append(line[at : at + part.size].reshape(part.shape))
        at += part.size
    return tuple(gathered)


def turned_gather(arrays, axis, dims):
    turned = [jnp.moveaxis(a, dim, 0) for a, dim in zip(arrays, dims)]
    widths = [t[0].size for t in turned]
    both = jnp.concatenate([t.reshape(-1, w) for t, w in zip(turned, widths)], axis=1)
    whole = lax.all_gather(both, axis, axis=0, tiled=True)
    blocks = jnp.split(whole, [sum(widths[:k]) for k in range(1, len(widths))], axis=1)
    return tuple(
        (
            jnp.moveaxis(b.reshape(-1, *t.shape[1:]), 0, dim)
            for b, t, dim in zip(blocks, turned, dims)
        )
    )


def on_device(
    grad_up,
    grad_down,
    grad_query,
    grad_key,
    grad_value,
    grad_mixed,
    grad_norm,
    weight_up,
    weight_down,
    weight_query,
    weight_key,
    weight_value,
    weight_mixed,
    weight_norm,
    moment_up,
    moment_down,
    moment_query,
    moment_key,
    moment_value,
    moment_mixed,
    moment_norm,
):
    mean_up, mean_down, mean_query, mean_key, mean_value, mean_mixed, mean_norm = one_scatter(
        (
            grad_up[0],
            grad_down[0],
            grad_query[0],
            grad_key[0],
            grad_value[0],
            grad_mixed[0],
            grad_norm[0],
        ),
        "data",
        (0, 1, 0, 0, 0, 1, 0),
    )
    mean_rate = lax.axis_size("data") ** (-0.5)
    mean_up = mean_up * mean_rate
    mean_down = mean_down * mean_rate
    mean_query = mean_query * mean_rate
    mean_key = mean_key * mean_rate
    mean_value = mean_value * mean_rate
    mean_mixed = mean_mixed * mean_rate
    mean_norm = mean_norm * mean_rate
    state_new_up = hold_rate * moment_up + (1.0 - hold_rate) * mean_up * mean_up
    new_up = weight_up - learn_rate * mean_up * lax.rsqrt(state_new_up + 1e-06)
    state_new_down = hold_rate * moment_down + (1.0 - hold_rate) * mean_down * mean_down
    new_down = weight_down - learn_rate * mean_down * lax.rsqrt(state_new_down + 1e-06)
    state_new_query = hold_rate * moment_query + (1.0 - hold_rate) * mean_query * mean_query
    new_query = weight_query - learn_rate * mean_query * lax.rsqrt(state_new_query + 1e-06)
    state_new_key = hold_rate * moment_key + (1.0 - hold_rate) * mean_key * mean_key
    new_key = weight_key - learn_rate * mean_key * lax.rsqrt(state_new_key + 1e-06)
    state_new_value = hold_rate * moment_value + (1.0 - hold_rate) * mean_value * mean_value
    new_value = weight_value - learn_rate * mean_value * lax.rsqrt(state_new_value + 1e-06)
    state_new_mixed = hold_rate * moment_mixed + (1.0 - hold_rate) * mean_mixed * mean_mixed
    new_mixed = weight_mixed - learn_rate * mean_mixed * lax.rsqrt(state_new_mixed + 1e-06)
    state_new_norm = hold_rate * moment_norm + (1.0 - hold_rate) * mean_norm * mean_norm
    new_norm = weight_norm - learn_rate * mean_norm * lax.rsqrt(state_new_norm + 1e-06)
    copy_up, copy_down, copy_query, copy_key, copy_value, copy_mixed, copy_norm = turned_gather(
        (
            new_up.astype(jnp.bfloat16),
            new_down.astype(jnp.bfloat16),
            new_query.astype(jnp.bfloat16),
            new_key.astype(jnp.bfloat16),
            new_value.astype(jnp.bfloat16),
            new_mixed.astype(jnp.bfloat16),
            new_norm.astype(jnp.bfloat16),
        ),
        "data",
        (0, 1, 0, 0, 0, 1, 0),
    )
    return (
        copy_up,
        copy_down,
        copy_query,
        copy_key,
        copy_value,
        copy_mixed,
        copy_norm,
        new_up,
        new_down,
        new_query,
        new_key,
        new_value,
        new_mixed,
        new_norm,
        state_new_up,
        state_new_down,
        state_new_query,
        state_new_key,
        state_new_value,
        state_new_mixed,
        state_new_norm,
    )


def solution(mesh):
    return jax.shard_map(
        on_device,
        mesh=mesh,
        in_specs=(
            P("data", None, "width"),
            P("data", "width", None),
            P("data", None, "width"),
            P("data", None, "width"),
            P("data", None, "width"),
            P("data", "width", None),
            P("data", None),
            P("data", "width"),
            P("width", "data"),
            P("data", "width"),
            P("data", "width"),
            P("data", "width"),
            P("width", "data"),
            P("data"),
            P("data", "width"),
            P("width", "data"),
            P("data", "width"),
            P("data", "width"),
            P("data", "width"),
            P("width", "data"),
            P("data"),
        ),
        out_specs=(
            P(None, "width"),
            P("width", None),
            P(None, "width"),
            P(None, "width"),
            P(None, "width"),
            P("width", None),
            P(),
            P("data", "width"),
            P("width", "data"),
            P("data", "width"),
            P("data", "width"),
            P("data", "width"),
            P("width", "data"),
            P("data"),
            P("data", "width"),
            P("width", "data"),
            P("data", "width"),
            P("data", "width"),
            P("data", "width"),
            P("width", "data"),
            P("data"),
        ),
        check_vma=False,
    )
```

profile of v0, /device:TPU:0, one launch (start us, length us, event | category | flops | bytes accessed | tf_op | source)
XLA Modules:
  0.0 577.1 jit_solution(8048873237569944627)
XLA Ops:
  7.2 2.0 copy.97
  9.3 6.6 %copy.98 = f32[32,768,24]{2,1,0:T(8,128)} copy(f32[32,768,24]{1,2,0:T(8,128)S(1)} %bitcast.19) | data formatting | bytes 4718592 | tf_op jit(solution)/shard_map/transpose | solution.py:13
  15.9 11.5 %reshape.120 = f32[32,18432]{1,0:T(8,128)} reshape(f32[32,768,24]{2,1,0:T(8,128)} %copy.98) | data formatting | bytes 4718592 | tf_op jit(solution)/shard_map/reshape | solution.py:19
  27.4 1.9 reshape_reshape_squeeze.12
  29.3 1.6 constant_dynamic-update-slice_fusion.6
  30.9 0.3 copy.99
  31.2 1.1 reshape_reshape_squeeze.13
  32.3 0.3 copy.100
  32.5 1.1 reshape_reshape_squeeze.14
  33.6 1.3 copy.101
  34.9 1.1 reshape_reshape_squeeze.15
  36.1 1.1 copy.102
  37.2 2.0 copy.103
  39.2 3.0 reshape.121
  42.3 3.3 constant_dynamic-update-slice_fusion.5
  45.6 2.0 constant_dynamic-update-slice_fusion.4
  47.6 1.9 constant_dynamic-update-slice_fusion.3
  49.6 0.9 constant_dynamic-update-slice_fusion.2
  50.4 0.9 constant_dynamic-update-slice_fusion.1
  51.3 0.6 constant_dynamic-update-slice_fusion
  51.9 6.4 %pad.4 = f32[32,56320]{1,0:T(8,128)} pad(f32[32,55320]{1,0:T(8,128)} %constant_dynamic-update-slice_fusion, f32[]{:T(128)} %constant.15.clone.1), padding=0_0x0_1000 | pad | bytes 14289924 | tf_op jit(solution)/shard_map/jit(_pad)/pad | solution.py:21
  58.3 6.8 %reshape.122 = f32[14080,128]{1,0:T(8,128)} reshape(f32[32,56320]{1,0:T(8,128)} %pad.4) | data formatting | bytes 14417920 | tf_op jit(solution)/shard_map/reshape | solution.py:21
  65.2 0.2 all-gather.2.cloned.1.call-start
  65.4 0.2 copy-done.20
  65.7 0.6 dynamic-slice
  66.9 406.0 %all-reduce.4.cloned.1.call-done = f32[14080,128]{1,0:T(8,128)} async-done(((f32[14080,128]{1,0:T(8,128)}), f32[14080,128]{1,0:T(8,128)}) %all-reduce.4.cloned.1.call-update) | async-done | bytes 7208976
  473.0 0.8 multiply_multiply_fusion.2
  474.6 1.0 multiply_multiply_fusion
  475.6 0.2 mul.225
  475.8 0.1 copy.104
  476.0 0.2 mul.219
  476.4 1.0 dynamic-slice_bitcast_fusion
  477.4 0.5 convert_bitcast_fusion.2
  478.0 0.6 convert_bitcast_fusion.1
  478.6 0.6 fusion.2
  479.3 0.7 convert_bitcast_fusion
  480.0 0.7 fusion.3
  480.7 0.6 fusion
  481.3 0.7 concatenate.7
  482.1 76.9 %all-gather.2.cloned.1.call-done = bf16[768,2305]{1,0:T(8,128)(2,1)} async-done(((bf16[24,2305]{1,0:T(8,128)(2,1)}), bf16[768,2305]{1,0:T(8,128)(2,1)}) %all-gather.2.cloned.1.call-update) | async-done | bytes 3540496 | tf_op jit(solution)/shard_map/all_gather | solution.py:34
  559.0 2.8 slice_bitcast_fusion
  561.8 1.4 copy.109
  563.2 1.9 slice_bitcast_fusion.1
  565.1 0.9 copy.110
  566.0 0.9 copy.111
  566.8 0.9 copy.112
  567.7 0.9 copy.113
  568.6 1.7 slice_reduce_fusion
  (60 shorter events, 1.3 us)
Async XLA Ops:
  7.2 465.8 %all-reduce.4.cloned.1.call-start = ((), (), s32[]{:S(2)}) async-start(), calls=%async_computation.1 | async-start | bytes 14417920
  27.4 3.5 copy-start.2
  27.4 4.8 copy-start.3
  30.9 5.1 copy-start.4
  32.3 10.0 %copy-start.17 = (f32[1,768]{1,0:T(1,128)S(1)}, f32[1,768]{1,0:T(1,128)}, u32[]{:S(2)}) copy-start(f32[1,768]{1,0:T(1,128)} %param.27) | copy-start | bytes 9220
  42.2 7.3 %copy-start.1 = (f32[32,4608]{1,0:T(8,128)S(1)}, f32[32,4608]{1,0:T(8,128)}, u32[]{:S(2)}) copy-start(f32[32,4608]{1,0:T(8,128)} %reshape_reshape_squeeze.15) | copy-start | bytes 1769476
  42.2 8.2 %copy-start = (f32[32,4608]{1,0:T(8,128)S(1)}, f32[32,4608]{1,0:T(8,128)}, u32[]{:S(2)}) copy-start(f32[32,4608]{1,0:T(8,128)} %reshape.121) | copy-start | bytes 1769476
  65.0 0.7 copy-start.20
  65.0 412.3 %copy-start.18 = (f32[24]{0:T(128)S(1)}, f32[24]{0:T(128)}, u32[]{:S(2)}) copy-start(f32[24]{0:T(128)} %param.34) | copy-start | bytes 292
  65.0 412.3 %copy-start.19 = (f32[24]{0:T(128)S(1)}, f32[24]{0:T(128)}, u32[]{:S(2)}) copy-start(f32[24]{0:T(128)} %param.41) | copy-start | bytes 292
  65.0 413.0 %copy-start.9 = (f32[192,24]{0,1:T(8,128)S(1)}, f32[192,24]{0,1:T(8,128)}, u32[]{:S(2)}) copy-start(f32[192,24]{0,1:T(8,128)} %param.33) | copy-start | bytes 55300
  65.1 413.0 %copy-start.10 = (f32[192,24]{0,1:T(8,128)S(1)}, f32[192,24]{0,1:T(8,128)}, u32[]{:S(2)}) copy-start(f32[192,24]{0,1:T(8,128)} %param.40) | copy-start | bytes 55300
  65.1 413.6 %copy-start.11 = (f32[24,192]{1,0:T(8,128)S(1)}, f32[24,192]{1,0:T(8,128)}, u32[]{:S(2)}) copy-start(f32[24,192]{1,0:T(8,128)} %param.30) | copy-start | bytes 55300
  65.1 413.6 %copy-start.12 = (f32[24,192]{1,0:T(8,128)S(1)}, f32[24,192]{1,0:T(8,128)}, u32[]{:S(2)}) copy-start(f32[24,192]{1,0:T(8,128)} %param.37) | copy-start | bytes 55300
  65.1 414.2 %copy-start.5 = (f32[768,24]{0,1:T(8,128)S(1)}, f32[768,24]{0,1:T(8,128)}, u32[]{:S(2)}) copy-start(f32[768,24]{0,1:T(8,128)} %param.29) | copy-start | bytes 221188
  65.1 414.2 %copy-start.6 = (f32[768,24]{0,1:T(8,128)S(1)}, f32[768,24]{0,1:T(8,128)}, u32[]{:S(2)}) copy-start(f32[768,24]{0,1:T(8,128)} %param.36) | copy-start | bytes 221188
  65.1 414.8 %copy-start.7 = (f32[24,768]{1,0:T(8,128)S(1)}, f32[24,768]{1,0:T(8,128)}, u32[]{:S(2)}) copy-start(f32[24,768]{1,0:T(8,128)} %param.28) | copy-start | bytes 221188
  65.1 414.8 %copy-start.8 = (f32[24,768]{1,0:T(8,128)S(1)}, f32[24,768]{1,0:T(8,128)}, u32[]{:S(2)}) copy-start(f32[24,768]{1,0:T(8,128)} %param.35) | copy-start | bytes 221188
  65.1 415.5 %copy-start.13 = (f32[24,192]{1,0:T(8,128)S(1)}, f32[24,192]{1,0:T(8,128)}, u32[]{:S(2)}) copy-start(f32[24,192]{1,0:T(8,128)} %param.32) | copy-start | bytes 55300
  65.1 415.5 %copy-start.14 = (f32[24,192]{1,0:T(8,128)S(1)}, f32[24,192]{1,0:T(8,128)}, u32[]{:S(2)}) copy-start(f32[24,192]{1,0:T(8,128)} %param.39) | copy-start | bytes 55300
  65.2 415.5 %copy-start.15 = (f32[24,192]{1,0:T(8,128)S(1)}, f32[24,192]{1,0:T(8,128)}, u32[]{:S(2)}) copy-start(f32[24,192]{1,0:T(8,128)} %param.31) | copy-start | bytes 55300
  65.2 415.5 %copy-start.16 = (f32[24,192]{1,0:T(8,128)S(1)}, f32[24,192]{1,0:T(8,128)}, u32[]{:S(2)}) copy-start(f32[24,192]{1,0:T(8,128)} %param.38) | copy-start | bytes 55300
  65.2 493.8 %all-gather.2.cloned.1.call-start = ((), (), s32[]{:S(2)}) async-start(), calls=%async_computation | async-start | bytes 3852288 | tf_op jit(solution)/shard_map/all_gather | solution.py:34
Sparse Core Ops, SparseCore 0:
  65.3 407.5 all-reduce.3
  482.2 76.7 all-gather.1
where the time goes:
time: 578 us; the launch traced here: 577 us
  waiting for transfers between devices  483 us (84%)
  local copies, waits for them, and re-layouts  73.2 us (13%)
  between operations  15 us (3%)
    unnamed x3, waiting for transfers between devices  406 us
    all_gather x1, waiting for transfers between devices, turned_gather(): whole = lax.all_gather(both, axis, axis=0, tiled=True)  76.9 us
    unnamed x59, local copies, waits for them, and re-layouts  21.4 us
    reshape x2, local copies, waits for them, and re-layouts, one_scatter(): lines = jnp.concatenate([b.reshape(devices, -1) for b in blocks], axis=1)  14.5 us
  transfers between devices with their start and end apart: 2, of which 2 were waited for; matrix products, arithmetic and copies ran while one was open for 0% of the time, Pallas kernels for 0%

commit v1 on v0

v1 whole, which is shorter than its diff:
```python
import jax
import jax.numpy as jnp
from jax import lax
from jax.experimental import pallas as pl
from jax.experimental.pallas import tpu as pltpu
from jax.sharding import PartitionSpec as P

learn_rate = 0.05
hold_rate = 0.9
mean_rate = 32 ** (-0.5)

MESH = pl.DeviceIdType.MESH
PIECES = 3
WIDE = 256
HALF = 128
UP, DOWN, MIXED = 0, 1, 2
FOLDED = (4, 4, 2, 24, WIDE)

SENDS = 36 * 3 + 28 * 6 + 7


def on_ring(step, size=4):
    return lax.rem(step, size)


class Place:
    def __init__(self):
        data, width = lax.axis_index("data"), lax.axis_index("width")
        self.z, self.y, self.xh = lax.div(data, 8), lax.rem(lax.div(data, 2), 4), lax.rem(data, 2)
        self.x, self.core = 2 * self.xh + lax.div(width, 2), lax.rem(width, 2)
        self.data = data

    def device(self, z, y, x):
        return (z * 8 + y * 2 + lax.div(x, 2), 2 * lax.rem(x, 2) + self.core)

    def along(self, axis, step):
        z, y, x = self.z, self.y, self.x
        if axis == "z":
            z = on_ring(z + step)
        elif axis == "y":
            y = on_ring(y + step)
        else:
            x = on_ring(x + step)
        return self.device(z, y, x)


class Sender:
    def __init__(self, place, send_sems, recv_sems):
        self.place, self.send_sems, self.recv_sems = place, send_sems, recv_sems
        self.copies = []

    def start(self, source, target, axis, step):
        n = len(self.copies)
        copy = pltpu.make_async_remote_copy(
            src_ref=source,
            dst_ref=target,
            send_sem=self.send_sems.at[n],
            recv_sem=self.recv_sems.at[n],
            device_id=self.place.along(axis, step),
            device_id_type=MESH,
        )
        copy.start()
        self.copies.append(copy)
        return copy

    def finish(self):
        for copy in self.copies:
            copy.wait_send()


def add_to(ref, *others):
    total = ref[...]
    for other in others:
        total = total + other[...]
    ref[...] = total


def ring_scatter(sender, block, axis, at, landing):
    plus, minus = on_ring(at + 1), on_ring(at + 3)
    opposite = on_ring(at + 2)
    far_plus = sender.start(block(opposite, 0), landing.at[0], axis, 1)
    far_minus = sender.start(block(opposite, 1), landing.at[1], axis, 3)
    near_plus = sender.start(block(plus, 1), landing.at[2], axis, 1)
    near_minus = sender.start(block(minus, 0), landing.at[3], axis, 3)
    yield
    far_plus.wait_recv()
    add_to(block(plus, 0), landing.at[0])
    both_plus = sender.start(block(plus, 0), landing.at[4], axis, 1)
    far_minus.wait_recv()
    add_to(block(minus, 1), landing.at[1])
    both_minus = sender.start(block(minus, 1), landing.at[5], axis, 3)
    yield
    near_minus.wait_recv()
    both_plus.wait_recv()
    add_to(block(at, 0), landing.at[3], landing.at[4])
    near_plus.wait_recv()
    both_minus.wait_recv()
    add_to(block(at, 1), landing.at[2], landing.at[5])


def ring_gather(sender, block, axis, at):
    plus, minus = on_ring(at + 1), on_ring(at + 3)
    first_plus = sender.start(block(at, 0), block(at, 0), axis, 1)
    first_minus = sender.start(block(at, 1), block(at, 1), axis, 3)
    second_plus = sender.start(block(at, 1), block(at, 1), axis, 1)
    second_minus = sender.start(block(at, 0), block(at, 0), axis, 3)
    yield
    first_plus.wait_recv()
    on_plus = sender.start(block(minus, 0), block(minus, 0), axis, 1)
    first_minus.wait_recv()
    on_minus = sender.start(block(plus, 1), block(plus, 1), axis, 3)
    yield
    for copy in (second_plus, second_minus, on_plus, on_minus):
        copy.wait_recv()


def updated(mean, weight, moment):
    state = hold_rate * moment + (1.0 - hold_rate) * mean * mean
    return weight - learn_rate * mean * lax.rsqrt(state + 1e-06), state


def stacked(block):
    return jnp.concatenate([block[:, :HALF], block[:, HALF:]], axis=0)


def exchange_kernel(*refs):
    (
        grad_up, grad_down, grad_query, grad_key, grad_value, grad_mixed, grad_norm,
        weight_up, weight_down, weight_query, weight_key, weight_value, weight_mixed, weight_norm,
        moment_up, moment_down, moment_query, moment_key, moment_value, moment_mixed, moment_norm,
        copy_up, copy_down, copy_query, copy_key, copy_value, copy_mixed, kept, norm_out,
        sums, turned, held, held_heads, whole, staged, kept_own, norm_own,
        pair_relay, pair_land, wide_land, thin_land,
        first_land, second_land, own_relay, own_land,
        copy_relay, copy_pair_relay,
        norm_grad, norm_held, norm_rows, norm_pair, norm_ring,
        send_sems, recv_sems, load_sems, store_sems,
    ) = refs
    place = Place()
    z, y, xh, x = place.z, place.y, place.xh, place.x
    far_xh = 1 - xh
    columns = [pl.ds(WIDE * k, WIDE) for k in range(PIECES)]

    loads = {}

    def load(name, source, target):
        copy = pltpu.make_async_copy(source, target, load_sems.at[len(loads)])
        copy.start()
        loads[name] = copy

    heads = (grad_query, grad_key, grad_value, grad_mixed)
    for k in range(PIECES):
        load(("up", k), grad_up.at[:, :, :, :, columns[k]], sums.at[UP, k])
        load(("down", k), grad_down.at[columns[k], :], turned.at[0, columns[k], :])
        for head in ((0, 1), (2,), (3,))[k]:
            load(("head", head), heads[head], turned.at[1, pl.ds(192 * head, 192), :])
    load("norm", grad_norm, norm_grad)
    load("weight_norm", weight_norm, norm_held.at[0])
    load("moment_norm", moment_norm, norm_held.at[1])
    load("weight_up", weight_up, held.at[0, UP])
    load("moment_up", moment_up, held.at[1, UP])
    load("weight_down", weight_down, held.at[0, DOWN])
    load("moment_down", moment_down, held.at[1, DOWN])
    for head, source in enumerate((weight_query, weight_key, weight_value, weight_mixed)):
        load(("weight", head), source, held_heads.at[0, head])
    for head, source in enumerate((moment_query, moment_key, moment_value, moment_mixed)):
        load(("moment", head), source, held_heads.at[1, head])

    barrier = pltpu.get_barrier_semaphore()
    for axis in ("x", "y", "z"):
        for step in (1, 2, 3):
            pl.semaphore_signal(barrier, inc=1, device_id=place.along(axis, step), device_id_type=MESH)
    pl.semaphore_wait(barrier, 9)

    sender = Sender(place, send_sems, recv_sems)
    stores = []

    def store(source, target):
        copy = pltpu.make_async_copy(source, target, store_sems.at[len(stores)])
        copy.start()
        stores.append(copy)

    def update_piece(part, k):
        own = sums[part, k, z, y, xh] * mean_rate
        new, state = updated(own, held[0, part, :, columns[k]], held[1, part, :, columns[k]])
        kept_own[0, part, :, columns[k]] = new
        kept_own[1, part, :, columns[k]] = state
        whole[part, k, z, y, xh] = stacked(new).astype(jnp.bfloat16)

    def up_stream(k):
        block = sums.at[UP, k]
        copied = whole.at[UP, k]
        second, third = ("y", "z") if k % 2 == 0 else ("z", "y")
        loads["up", k].wait()
        sent = [
            sender.start(block.at[pl.ds(2 * h, 2), :, far_xh], pair_relay.at[k, h], "x", (1, 3)[h])
            for h in range(2)
        ]
        yield
        on = []
        for h in range(2):
            sent[h].wait_recv()
            on.append(sender.start(pair_relay.at[k, h], pair_land.at[k, h], "x", (1, 3)[h]))
        yield
        for h in range(2):
            on[h].wait_recv()
            add_to(block.at[pl.ds(2 * h, 2), :, xh], pair_land.at[k, h])
        if second == "y":
            yield from ring_scatter(
                sender, lambda q, h: block.at[pl.ds(2 * h, 2), q, xh], "y", y, wide_land.at[k]
            )
            yield from ring_scatter(
                sender, lambda q, h: block.at[q, y, xh, :, pl.ds(HALF * h, HALF)], "z", z, thin_land.at[k]
            )
        else:
            yield from ring_scatter(
                sender, lambda q, h: block.at[q, pl.ds(2 * h, 2), xh], "z", z, wide_land.at[k]
            )
            yield from ring_scatter(
                sender, lambda q, h: block.at[z, q, xh, :, pl.ds(HALF * h, HALF)], "y", y, thin_land.at[k]
            )
        if k == 0:
            loads["weight_up"].wait()
            loads["moment_up"].wait()
        update_piece(UP, k)
        rows = (pl.ds(0, 32), pl.ds(32, 16))
        if second == "y":
            yield from ring_gather(sender, lambda q, h: copied.at[q, y, xh, rows[h], :], "z", z)
            yield from ring_gather(sender, lambda q, h: copied.at[pl.ds(2 * h, 2), q, xh], "y", y)
        else:
            yield from ring_gather(sender, lambda q, h: copied.at[z, q, xh, rows[h], :], "y", y)
            yield from ring_gather(sender, lambda q, h: copied.at[q, pl.ds(2 * h, 2), xh], "z", z)
        sent = [
            sender.start(copied.at[pl.ds(2 * h, 2), :, xh], copy_pair_relay.at[k, h], "x", (1, 3)[h])
            for h in range(2)
        ]
        yield
        on = []
        for h in range(2):
            sent[h].wait_recv()
            origin = lax.div(on_ring(x + (3, 1)[h]), 2)
            on.append(
                sender.start(
                    copy_pair_relay.at[k, h], copied.at[pl.ds(2 * h, 2), :, origin], "x", (1, 3)[h]
                )
            )
        yield
        for h in range(2):
            on[h].wait_recv()

        def pair_of_chunks(n, carry):
            chunks = [
                copied[lax.div(n, 4), lax.rem(n, 4), side].astype(jnp.float32) for side in range(2)
            ]
            at = pl.ds(pl.multiple_of(48 * n, 16), 48)
            for half in range(2):
                both = jnp.concatenate([c[24 * half : 24 * half + 24] for c in chunks], axis=0)
                staged[UP, at, pl.ds(WIDE * k + HALF * half, HALF)] = both.astype(jnp.bfloat16)
            return carry

        lax.fori_loop(0, 16, pair_of_chunks, 0)
        store(staged.at[UP, :, columns[k]], copy_up.at[:, columns[k]])

    def turned_stream(part, k):
        block = sums.at[part, k]
        copied = whole.at[part, k]
        step = (1, 3)[part - 1]
        if part == DOWN:
            loads["down", k].wait()
        else:
            for head in ((0, 1), (2,), (3,))[k]:
                loads["head", head].wait()

        def turn(n, carry):
            lanes = pl.ds(pl.multiple_of(384 * n, HALF), 384)
            tile = turned[part - 1, columns[k], lanes]
            block[pl.ds(2 * n, 2)] = tile.T.reshape(2, 4, 2, 24, WIDE)
            return carry

        lax.fori_loop(0, 2, turn, 0)
        if part == DOWN:
            yield from ring_scatter(
                sender, lambda q, h: block.at[q, pl.ds(2 * h, 2)], "z", z, first_land.at[part - 1, k]
            )
            yield from ring_scatter(
                sender, lambda q, h: block.at[z, q, h], "y", y, second_land.at[part - 1, k]
            )
        else:
            yield from ring_scatter(
                sender, lambda q, h: block.at[pl.ds(2 * h, 2), q], "y", y, first_land.at[part - 1, k]
            )
            yield from ring_scatter(
                sender, lambda q, h: block.at[q, y, h], "z", z, second_land.at[part - 1, k]
            )
        sent = sender.start(block.at[z, y, far_xh], own_relay.at[part - 1, k], "x", step)
        yield
        sent.wait_recv()
        on = sender.start(own_relay.at[part - 1, k], own_land.at[part - 1, k], "x", step)
        yield
        on.wait_recv()
        add_to(block.at[z, y, xh], own_land.at[part - 1, k])
        if k == 0:
            if part == DOWN:
                loads["weight_down"].wait()
                loads["moment_down"].wait()
            else:
                for row, name in enumerate(("weight", "moment")):
                    for head in range(4):
                        loads[name, head].wait()
                    held[row, part] = jnp.concatenate([held_heads[row, head] for head in range(4)], axis=1)
        update_piece(part, k)
        sent = sender.start(copied.at[z, y, xh], copy_relay.at[part - 1, k], "x", step)
        yield
        sent.wait_recv()
        origin = lax.div(on_ring(x + 4 - step), 2)
        on = sender.start(copy_relay.at[part - 1, k], copied.at[z, y, origin], "x", step)
        yield
        on.wait_recv()
        if part == DOWN:
            yield from ring_gather(sender, lambda q, h: copied.at[z, q, h], "y", y)
            yield from ring_gather(sender, lambda q, h: copied.at[q, pl.ds(2 * h, 2)], "z", z)
        else:
            yield from ring_gather(sender, lambda q, h: copied.at[q, y, h], "z", z)
            yield from ring_gather(sender, lambda q, h: copied.at[pl.ds(2 * h, 2), q], "y", y)
        for half in range(2):
            tile = copied[:, :, :, 24 * half : 24 * half + 24, :].astype(jnp.float32)
            staged[part, WIDE * k + HALF * half : WIDE * k + HALF * half + HALF, :] = (
                tile.reshape(768, HALF).T.astype(jnp.bfloat16)
            )
        if part == DOWN:
            store(staged.at[DOWN, columns[k], :], copy_down.at[columns[k], :])
        else:
            for head in ((0,), (1,), (2, 3))[k]:
                store(
                    staged.at[MIXED, pl.ds(192 * head, 192), :],
                    (copy_query, copy_key, copy_value, copy_mixed)[head],
                )

    def norm_stream():
        for name in ("norm", "weight_norm", "moment_norm"):
            loads[name].wait()
        norm_rows[...] = jnp.zeros_like(norm_rows)
        norm_rows[1:2, 0:24] = norm_held[0]
        norm_rows[2:3, 0:24] = norm_held[1]
        placed = pltpu.roll(norm_rows[...], 24 * place.data, 1)
        row = lax.broadcasted_iota(jnp.int32, (8, 768), 0)
        norm_pair[xh] = jnp.where(row == 0, jnp.broadcast_to(norm_grad[...], (8, 768)), placed)
        copy = sender.start(norm_pair.at[xh], norm_pair.at[xh], "x", 2)
        yield
        copy.wait_recv()
        norm_ring[0, y] = norm_pair[0] + norm_pair[1]
        copies = [sender.start(norm_ring.at[0, y], norm_ring.at[0, y], "y", s) for s in (1, 2, 3)]
        yield
        for copy in copies:
            copy.wait_recv()
        norm_ring[1, z] = norm_ring[0, 0] + norm_ring[0, 1] + norm_ring[0, 2] + norm_ring[0, 3]
        copies = [sender.start(norm_ring.at[1, z], norm_ring.at[1, z], "z", s) for s in (1, 2, 3)]
        yield
        for copy in copies:
            copy.wait_recv()
        total = norm_ring[1, 0] + norm_ring[1, 1] + norm_ring[1, 2] + norm_ring[1, 3]
        new, state = updated(total[0:1] * mean_rate, total[1:2], total[2:3])
        norm_rows[0:1] = new
        norm_rows[1:2] = state
        norm_own[0] = norm_rows[...]
        norm_own[1] = pltpu.roll(norm_rows[...], lax.rem(768 - 24 * place.data, 768), 1)
        store(norm_own, norm_out)

    streams = {}
    for k in range(PIECES):
        streams[UP, k] = up_stream(k)
        streams[DOWN, k] = turned_stream(DOWN, k)
        streams[MIXED, k] = turned_stream(MIXED, k)
    streams["norm"] = norm_stream()
    for name in ORDER:
        next(streams[name], None)
    store(kept_own, kept)
    for copy in stores:
        copy.wait()
    sender.finish()


def default_order():
    order = []
    for step in range(13 + 2 * 2):
        for k in range(PIECES):
            phase = step - 2 * k
            if 0 <= phase < 13:
                order += [(UP, k), (DOWN, k), (MIXED, k)]
        if 1 <= step < 5:
            order.append("norm")
    return tuple(order)


ORDER = default_order()


def split_kernel(*refs):
    (
        copy_up, copy_down, copy_query, copy_key, copy_value, copy_mixed, kept, norm_out,
        o_copy_up, o_copy_down, o_copy_query, o_copy_key, o_copy_value, o_copy_mixed, o_copy_norm,
        o_new_up, o_new_down, o_new_query, o_new_key, o_new_value, o_new_mixed, o_new_norm,
        o_state_up, o_state_down, o_state_query, o_state_key, o_state_value, o_state_mixed, o_state_norm,
    ) = refs
    for source, target in (
        (copy_up, o_copy_up),
        (copy_down, o_copy_down),
        (copy_query, o_copy_query),
        (copy_key, o_copy_key),
        (copy_value, o_copy_value),
        (copy_mixed, o_copy_mixed),
    ):
        target[...] = source[...]
    o_copy_norm[...] = norm_out[0, 0:1].astype(jnp.bfloat16)
    for row, targets in enumerate(
        (
            (o_new_up, o_new_down, o_new_query, o_new_key, o_new_value, o_new_mixed),
            (o_state_up, o_state_down, o_state_query, o_state_key, o_state_value, o_state_mixed),
        )
    ):
        targets[0][...] = kept[row, UP]
        targets[1][...] = kept[row, DOWN]
        heads = kept[row, MIXED]
        for head in range(4):
            targets[2 + head][...] = heads[:, 192 * head : 192 * head + 192]
    o_new_norm[...] = norm_out[1, 0:1, 0:24]
    o_state_norm[...] = norm_out[1, 1:2, 0:24]


def on_device(
    grad_up, grad_down, grad_query, grad_key, grad_value, grad_mixed, grad_norm,
    weight_up, weight_down, weight_query, weight_key, weight_value, weight_mixed, weight_norm,
    moment_up, moment_down, moment_query, moment_key, moment_value, moment_mixed, moment_norm,
):
    f32, bf16 = jnp.float32, jnp.bfloat16
    anywhere = pl.BlockSpec(memory_space=pl.ANY)
    shape = jax.ShapeDtypeStruct
    operands = (
        grad_up[0].reshape(4, 4, 2, 24, 768), grad_down[0],
        grad_query[0].T, grad_key[0].T, grad_value[0].T, grad_mixed[0], grad_norm,
        weight_up, weight_down.T, weight_query, weight_key, weight_value, weight_mixed.T, weight_norm[None],
        moment_up, moment_down.T, moment_query, moment_key, moment_value, moment_mixed.T, moment_norm[None],
    )
    copy_shapes = (shape((768, 768), bf16),) * 2 + (shape((192, 768), bf16),) * 4
    gathered = pl.pallas_call(
        exchange_kernel,
        name="exchange",
        out_shape=copy_shapes + (shape((2, 3, 24, 768), f32), shape((2, 8, 768), f32)),
        in_specs=[anywhere] * 21,
        out_specs=[anywhere] * 8,
        scratch_shapes=[
            pltpu.VMEM((3, PIECES) + FOLDED, f32),
            pltpu.VMEM((2, 768, 768), f32),
            pltpu.VMEM((2, 3, 24, 768), f32),
            pltpu.VMEM((2, 4, 24, 192), f32),
            pltpu.VMEM((3, PIECES, 4, 4, 2, 48, HALF), bf16),
            pltpu.VMEM((3, 768, 768), bf16),
            pltpu.VMEM((2, 3, 24, 768), f32),
            pltpu.VMEM((2, 8, 768), f32),
            pltpu.VMEM((PIECES, 2, 2, 4, 24, WIDE), f32),
            pltpu.VMEM((PIECES, 2, 2, 4, 24, WIDE), f32),
            pltpu.VMEM((PIECES, 6, 2, 24, WIDE), f32),
            pltpu.VMEM((PIECES, 6, 24, HALF), f32),
            pltpu.VMEM((2, PIECES, 6, 2, 2, 24, WIDE), f32),
            pltpu.VMEM((2, PIECES, 6, 24, WIDE), f32),
            pltpu.VMEM((2, PIECES, 24, WIDE), f32),
            pltpu.VMEM((2, PIECES, 24, WIDE), f32),
            pltpu.VMEM((2, PIECES, 48, HALF), bf16),
            pltpu.VMEM((PIECES, 2, 2, 4, 48, HALF), bf16),
            pltpu.VMEM((1, 768), f32),
            pltpu.VMEM((2, 1, 24), f32),
            pltpu.VMEM((8, 768), f32),
            pltpu.VMEM((2, 8, 768), f32),
            pltpu.VMEM((2, 4, 8, 768), f32),
            pltpu.SemaphoreType.DMA((SENDS,)),
            pltpu.SemaphoreType.DMA((SENDS,)),
            pltpu.SemaphoreType.DMA((28,)),
            pltpu.SemaphoreType.DMA((12,)),
        ],
        compiler_params=pltpu.CompilerParams(collective_id=0, has_side_effects=True),
    )(*operands)
    kept_shapes = (
        (shape((24, 768), f32),) * 2 + (shape((24, 192), f32),) * 4 + (shape((1, 24), f32),)
    )
    outs = pl.pallas_call(
        split_kernel,
        name="split",
        out_shape=copy_shapes + (shape((1, 768), bf16),) + kept_shapes * 2,
    )(*gathered)
    copy_up, copy_down, copy_query, copy_key, copy_value, copy_mixed, copy_norm = outs[:7]

    def as_given(seven):
        up, down, query, key, value, mixed, norm = seven
        return (up, down.T, query, key, value, mixed.T, norm[0])

    return (
        (copy_up, copy_down, copy_query.T, copy_key.T, copy_value.T, copy_mixed, copy_norm[0])
        + as_given(outs[7:14])
        + as_given(outs[14:])
    )


def solution(mesh):
    return jax.shard_map(
        on_device,
        mesh=mesh,
        in_specs=(
            P("data", None, "width"),
            P("data", "width", None),
            P("data", None, "width"),
            P("data", None, "width"),
            P("data", None, "width"),
            P("data", "width", None),
            P("data", None),
        )
        + (
            P("data", "width"),
            P("width", "data"),
            P("data", "width"),
            P("data", "width"),
            P("data", "width"),
            P("width", "data"),
            P("data"),
        )
        * 2,
        out_specs=(
            P(None, "width"),
            P("width", None),
            P(None, "width"),
            P(None, "width"),
            P(None, "width"),
            P("width", None),
            P(),
        )
        + (
            P("data", "width"),
            P("width", "data"),
            P("data", "width"),
            P("data", "width"),
            P("data", "width"),
            P("width", "data"),
            P("data"),
        )
        * 2,
        check_vma=False,
    )
```

time: 578 us -> 99.1 us (0.17)
  waiting for transfers between devices: 483 us -> 0 us
  Pallas kernels: 0 us -> 97 us
  local copies, waits for them, and re-layouts: 73.2 us -> 0 us
  between operations: 15 us -> 0.68 us
    unnamed x3 -> x0, waiting for transfers between devices: 406 us -> none
    pallas_call x0 -> x2, Pallas kernels: none -> 97 us  [the longest x1 92.9 us: on_device(): pl.pallas_call(exchange_kernel, name='exchange', out_shape=copy_shapes +...]
    all_gather x1 -> x0, waiting for transfers between devices: 76.9 us -> none  [turned_gather(): whole = lax.all_gather(both, axis, axis=0, tiled=True)]
    reshape x5 -> x0, local copies, waits for them, and re-layouts: 22.3 us -> none  [the longest x2 14.5 us: one_scatter(): lines = jnp.concatenate([b.reshape(devices, -1) for b in blocks], axis=1)]
    unnamed x59 -> x0, local copies, waits for them, and re-layouts: 21.4 us -> none
    transpose x4 -> x0, local copies, waits for them, and re-layouts: 13.3 us -> none  [the longest x2 8.66 us: in_blocks(): return jnp.moveaxis(blocks, dim, 0)]
    pad x1 -> x0, local copies, waits for them, and re-layouts: 6.39 us -> none  [one_scatter(): jnp.pad(lines, ((0, 0), (0, span * 128 - lines.shape[1]))).reshape(-1, 128)]
  transfers between devices with their start and end apart: 2 -> 0, of which waited for: 2 -> 0; matrix products, arithmetic and copies ran while one was open for 0% -> 0% of each run, Pallas kernels for 0% -> 0%
where the time goes in v1:
time: 99.1 us; the launch traced here: 99 us
  Pallas kernels  97 us (98%)
  other arithmetic  1.28 us (1%)
    pallas_call x1, Pallas kernels, on_device(): pl.pallas_call(exchange_kernel, name='exchange', out_shape=copy_shapes +...  92.9 us
    pallas_call x1, Pallas kernels, on_device(): pl.pallas_call(split_kernel, name='split', out_shape=copy_shapes + (shape...  4.12 us

profile of v1, /device:TPU:0, one launch (start us, length us, event | category | flops | bytes accessed | tf_op | source)
XLA Modules:
  0.0 99.0 jit_solution(8663686916892657926)
XLA Ops:
  0.7 92.9 %exchange.1 = (bf16[768,768]{1,0:T(8,128)(2,1)}, bf16[768,768]{1,0:T(8,128)(2,1)}, bf16[192,768]{1,0:T(8,128)(2,1)}, bf16[192,768]{1,0:T(8,128)(2,1)}, bf16[192,...) custom-call(f32[4,4,2,24,768]{4,3,2,1,0:T(8,128)} %bitcast.27, ...), custom_call_target="tpu_custom_call" | custom-call | tf_op jit(solution)/shard_map/exchange/pallas_call | solution.py:445
  93.6 4.1 %split.1 = (bf16[768,768]{1,0:T(8,128)(2,1)}, bf16[768,768]{1,0:T(8,128)(2,1)}, bf16[192,768]{1,0:T(8,128)(2,1)}, bf16[192,768]{1,0:T(8,128)(2,1)}, bf16[192,768...) custom-call(bf16[768,768]{1,0:T(8,128)(2,1)} %get-tuple-element.50.r, ...), custom_call_target="tpu_custom_call" | custom-call | tf_op jit(solution)/shard_map/split/pallas_call | solution.py:485
  97.7 1.3 %reduce = bf16[768]{0:T(1024)(128)(2,1)} reduce(bf16[1,768]{1,0:T(2,128)(2,1)} %get-tuple-element.64, bf16[]{:T(256)} %constant.21), dimensions={0}, to_apply=%get-tuple-element.64.reduce_sub_computation | reduce | bytes 3074 | tf_op jit(solution)/shard_map/split/pallas_call | solution.py:485

commit v2 on v1

v2 whole, which is shorter than its diff:
```python
import jax
import jax.numpy as jnp
from jax import lax
from jax.experimental import pallas as pl
from jax.experimental.pallas import tpu as pltpu
from jax.sharding import PartitionSpec as P

learn_rate = 0.05
hold_rate = 0.9
mean_rate = 32 ** (-0.5)

MESH = pl.DeviceIdType.MESH
WIDE = 256
HALF = 128
UP, DOWN, MIXED = 0, 1, 2
FOLDED = (4, 4, 2, 24, WIDE)
BLOCKS = 3
RAW = 6.0
SENDS = 196
STREAMS = (
    (UP, 0, 0, 24, "xyz", "dtd", "ddd"),
    (DOWN, 0, 0, 24, "zyx", "ttd", "tdd"),
    (MIXED, 0, 0, 24, "yzx", "ttd", "tdd"),
    (UP, 1, 0, 24, "xzy", "dtd", "ddd"),
    (DOWN, 1, 0, 24, "zyx", "ttd", "tdd"),
    (MIXED, 1, 0, 24, "yzx", "ttd", "tdd"),
    (UP, 2, 0, 24, "xyz", "dtd", "ddd"),
    (DOWN, 2, 0, 24, "zyx", "ttd", "tdd"),
    (MIXED, 2, 0, 24, "yzx", "ttd", "tdd"),
)
ORDER = (
    0, 1, 2, 3, 4, 5, 6, 7, 8, 9, 1, 2, 4, 5, 0, 7, 8, 1, 2, 4, 3, 5, 0, 7,
    2, 8, 1, 3, 4, 5, 6, 9, 0, 2, 7, 8, 1, 4, 3, 5, 6, 2, 0, 8, 9, 7, 1, 4,
    3, 5, 6, 2, 0, 9, 8, 7, 1, 4, 3, 5, 6, 8, 2, 7, 0, 1, 4, 3, 5, 2, 6, 8,
    7, 1, 5, 0, 4, 2, 7, 6, 3, 1, 8, 4, 7, 5, 8, 6,
)


def on_ring(step, size=4):
    return lax.rem(step, size)


class Place:
    def __init__(self):
        data, width = lax.axis_index("data"), lax.axis_index("width")
        self.z, self.y, self.xh = lax.div(data, 8), lax.rem(lax.div(data, 2), 4), lax.rem(data, 2)
        self.x, self.core = 2 * self.xh + lax.div(width, 2), lax.rem(width, 2)
        self.data = data

    def device(self, z, y, x):
        return (z * 8 + y * 2 + lax.div(x, 2), 2 * lax.rem(x, 2) + self.core)

    def along(self, axis, step):
        z, y, x = self.z, self.y, self.x
        if axis == "z":
            z = on_ring(z + step)
        elif axis == "y":
            y = on_ring(y + step)
        else:
            x = on_ring(x + step)
        return self.device(z, y, x)


class Sender:
    def __init__(self, place, send_sems, recv_sems):
        self.place, self.send_sems, self.recv_sems = place, send_sems, recv_sems
        self.copies = []

    def start(self, source, target, axis, step):
        n = len(self.copies)
        copy = pltpu.make_async_remote_copy(
            src_ref=source,
            dst_ref=target,
            send_sem=self.send_sems.at[n],
            recv_sem=self.recv_sems.at[n],
            device_id=self.place.along(axis, step),
            device_id_type=MESH,
        )
        copy.start()
        self.copies.append(copy)
        return copy

    def finish(self):
        for copy in self.copies:
            copy.wait_send()


def add_to(ref, *others):
    total = ref[...]
    for other in others:
        total = total + other[...]
    ref[...] = total


class Lines:
    def __init__(self, place, axes):
        self.at = {"z": place.z, "y": place.y, "x": place.xh}
        self.axes = axes

    def chosen(self, stage, q, half=None):
        index = dict(z=slice(None), y=slice(None), x=slice(None))
        for axis in self.axes[:stage]:
            index[axis] = self.at[axis]
        index[self.axes[stage]] = q
        if half is not None:
            split = self.axes[stage + 1] if self.axes[stage + 1] != "x" else self.axes[-1]
            index[split] = half if split == "x" else pl.ds(2 * half, 2)
        return index["z"], index["y"], index["x"]

    def span(self, stage, halved=False):
        sizes = dict(z=4, y=4, x=2)
        left = list(self.axes[stage + 1 :])
        shape = []
        split = None
        if halved:
            split = self.axes[stage + 1] if self.axes[stage + 1] != "x" else self.axes[-1]
        for axis in "zyx":
            if axis in left:
                if axis == split:
                    if axis != "x":
                        shape.append(2)
                else:
                    shape.append(sizes[axis])
        return tuple(shape)


def encode(values, largest):
    first = jnp.floor(values[:3] * ((2**18 - 1) / largest) + 0.5) * 64.0
    fourth = jnp.floor(values[3] * ((2**17 - 1) / largest) + (2**17 + 0.5))
    high = jnp.floor(fourth * 2.0**-12)
    rest = fourth - high * 4096.0
    middle = jnp.floor(rest * 2.0**-6)
    return first + jnp.stack([high, middle, rest - middle * 64.0])


def decode(coded, largest):
    first = jnp.floor(coded * 2.0**-6)
    digits = coded - first * 64.0
    fourth = (digits[0] * 64.0 + digits[1]) * 64.0 + (digits[2] - 2.0**17)
    return jnp.concatenate(
        [first * (largest / (2**18 - 1)), (fourth * (largest / (2**17 - 1)))[None]], axis=0
    )


def fours(ref):
    return ref[...].reshape((4,) + ref.shape[-2:])


def coded_stage(sender, lines, block, coded, landing):
    axis = lines.axes[0]
    at = lines.at[axis]
    if axis == "x":
        far = block(*lines.chosen(0, 1 - at))
        own = block(*lines.chosen(0, at))
        for n in range(4):
            coded[n] = encode(far[n], RAW)
        copy = sender.start(coded, landing, axis, 2)
        yield
        copy.wait_recv()
        for n in range(4):
            own[n] = own[n] + decode(landing[n], RAW)
        return
    plus, minus, opposite = on_ring(at + 1), on_ring(at + 3), on_ring(at + 2)

    def part(q, half):
        return block(*lines.chosen(0, q, half))

    def send(n, values, largest, step):
        coded[n] = encode(values, largest)
        return sender.start(coded.at[n], landing.at[n], axis, step)

    far_plus = send(0, fours(part(opposite, 0)), RAW, 1)
    far_minus = send(1, fours(part(opposite, 1)), RAW, 3)
    near_plus = send(2, fours(part(plus, 1)), RAW, 1)
    near_minus = send(3, fours(part(minus, 0)), RAW, 3)
    yield
    far_plus.wait_recv()
    both_plus = send(4, fours(part(plus, 0)) + decode(landing[0], RAW), 2 * RAW, 1)
    far_minus.wait_recv()
    both_minus = send(5, fours(part(minus, 1)) + decode(landing[1], RAW), 2 * RAW, 3)
    yield
    for near, near_slot, both, both_slot, half in (
        (near_minus, 3, both_plus, 4, 0),
        (near_plus, 2, both_minus, 5, 1),
    ):
        near.wait_recv()
        both.wait_recv()
        own = part(at, half)
        total = fours(own) + decode(landing[near_slot], RAW) + decode(landing[both_slot], 2 * RAW)
        own[...] = total.reshape(own.shape)


def scatter_stage(sender, lines, stage, mode, block, landing):
    axis = lines.axes[stage]
    at = lines.at[axis]
    own = block(*lines.chosen(stage, at))
    if axis == "x":
        copy = sender.start(block(*lines.chosen(stage, 1 - at)), landing.at[0], axis, 2)
        yield
        copy.wait_recv()
        add_to(own, landing.at[0])
        return
    plus, minus, opposite = on_ring(at + 1), on_ring(at + 3), on_ring(at + 2)
    if mode == "d":
        copies = [
            sender.start(block(*lines.chosen(stage, q)), landing.at[n], axis, step)
            for n, (q, step) in enumerate(((opposite, 2), (plus, 1), (minus, 3)))
        ]
        yield
        for copy in copies:
            copy.wait_recv()
        add_to(own, *(landing.at[n] for n in range(3)))
        return

    def part(q, half):
        return block(*lines.chosen(stage, q, half))

    far_plus = sender.start(part(opposite, 0), landing.at[0], axis, 1)
    far_minus = sender.start(part(opposite, 1), landing.at[1], axis, 3)
    near_plus = sender.start(part(plus, 1), landing.at[2], axis, 1)
    near_minus = sender.start(part(minus, 0), landing.at[3], axis, 3)
    yield
    far_plus.wait_recv()
    add_to(part(plus, 0), landing.at[0])
    both_plus = sender.start(part(plus, 0), landing.at[4], axis, 1)
    far_minus.wait_recv()
    add_to(part(minus, 1), landing.at[1])
    both_minus = sender.start(part(minus, 1), landing.at[5], axis, 3)
    yield
    near_minus.wait_recv()
    both_plus.wait_recv()
    add_to(part(at, 0), landing.at[3], landing.at[4])
    near_plus.wait_recv()
    both_minus.wait_recv()
    add_to(part(at, 1), landing.at[2], landing.at[5])


def gather_stage(sender, lines, stage, mode, block):
    axis = lines.axes[stage]
    at = lines.at[axis]
    own = block(*lines.chosen(stage, at))
    if axis == "x" or mode == "d":
        copies = [sender.start(own, own, axis, step) for step in ((2,) if axis == "x" else (2, 1, 3))]
        yield
        for copy in copies:
            copy.wait_recv()
        return

    def part(q, half):
        return block(*lines.chosen(stage, q, half))

    plus, minus = on_ring(at + 1), on_ring(at + 3)
    first_plus = sender.start(part(at, 0), part(at, 0), axis, 1)
    first_minus = sender.start(part(at, 1), part(at, 1), axis, 3)
    second_plus = sender.start(part(at, 1), part(at, 1), axis, 1)
    second_minus = sender.start(part(at, 0), part(at, 0), axis, 3)
    yield
    first_plus.wait_recv()
    on_plus = sender.start(part(minus, 0), part(minus, 0), axis, 1)
    first_minus.wait_recv()
    on_minus = sender.start(part(plus, 1), part(plus, 1), axis, 3)
    yield
    for copy in (second_plus, second_minus, on_plus, on_minus):
        copy.wait_recv()


def updated(mean, weight, moment):
    state = hold_rate * moment + (1.0 - hold_rate) * mean * mean
    return weight - learn_rate * mean * lax.rsqrt(state + 1e-06), state


def exchange_kernel(*refs):
    (
        grad_up, grad_down, grad_query, grad_key, grad_value, grad_mixed, grad_norm,
        weight_up, weight_down, weight_query, weight_key, weight_value, weight_mixed, weight_norm,
        moment_up, moment_down, moment_query, moment_key, moment_value, moment_mixed, moment_norm,
        out_up, out_down, out_mixed, norm_all,
        new_up, new_down, new_query, new_key, new_value, new_mixed, new_norm,
        state_up, state_down, state_query, state_key, state_value, state_mixed, state_norm,
        sums, turned, held, held_heads, whole, mixed_own,
        norm_grad, norm_held, norm_rows, norm_pair, norm_ring,
        send_sems, recv_sems, load_sems,
        *landings,
    ) = refs
    place = Place()
    z, y, xh = place.z, place.y, place.xh
    columns = [pl.ds(WIDE * k, WIDE) for k in range(BLOCKS)]

    barrier = pltpu.get_barrier_semaphore()
    for axis in ("x", "y", "z"):
        for step in (2,) if axis == "x" else (1, 2, 3):
            pl.semaphore_signal(barrier, inc=1, device_id=place.along(axis, step), device_id_type=MESH)

    loads = {}

    def load(name, source, target):
        copy = pltpu.make_async_copy(source, target, load_sems.at[len(loads)])
        copy.start()
        loads[name] = copy

    heads = (grad_query, grad_key, grad_value, grad_mixed)
    for k in range(BLOCKS):
        load((UP, k), grad_up.at[:, :, :, :, columns[k]], sums.at[UP, k])
        load((DOWN, k), grad_down.at[columns[k], :], turned.at[0, columns[k], :])
        for head in ((0, 1), (2,), (3,))[k]:
            load(("head", head), heads[head], turned.at[1, pl.ds(192 * head, 192), :])
    load("norm", grad_norm, norm_grad)
    load("weight_norm", weight_norm, norm_held.at[0])
    load("moment_norm", moment_norm, norm_held.at[1])
    load(("weight", UP), weight_up, held.at[0, UP])
    load(("moment", UP), moment_up, held.at[1, UP])
    load(("weight", DOWN), weight_down, held.at[0, DOWN])
    load(("moment", DOWN), moment_down, held.at[1, DOWN])
    for head, source in enumerate((weight_query, weight_key, weight_value, weight_mixed)):
        load(("weight head", head), source, held_heads.at[0, head])
    for head, source in enumerate((moment_query, moment_key, moment_value, moment_mixed)):
        load(("moment head", head), source, held_heads.at[1, head])

    sender = Sender(place, send_sems, recv_sems)
    gathered = {}
    ready = set()

    def make_ready(part, k):
        if (part, k) in ready:
            return
        ready.add((part, k))
        if part == UP:
            loads[UP, k].wait()
            return
        if part == DOWN:
            loads[DOWN, k].wait()
        else:
            for head in ((0, 1), (2,), (3,))[k]:
                loads["head", head].wait()

        def turn(n, carry):
            lanes = pl.ds(pl.multiple_of(384 * n, HALF), 384)
            tile = turned[part - 1, columns[k], lanes]
            sums[part, k, pl.ds(2 * n, 2)] = tile.T.reshape(2, 4, 2, 24, WIDE)
            return carry

        lax.fori_loop(0, 2, turn, 0)

    def hold(part):
        if ("held", part) in ready:
            return
        ready.add(("held", part))
        if part != MIXED:
            loads["weight", part].wait()
            loads["moment", part].wait()
            return
        for row, name in enumerate(("weight head", "moment head")):
            for head in range(4):
                loads[name, head].wait()
            held[row, part] = jnp.concatenate([held_heads[row, head] for head in range(4)], axis=1)

    def finish(part, k, rows):
        done = gathered.setdefault((part, k), [])
        done.append(rows)
        if sum(count for _, count in done) < 24:
            return
        done.sort()

        def side(chunk, half):
            return [
                chunk[..., 2 * first + count * half : 2 * first + count * half + count, :]
                for first, count in done
            ]

        if part == UP:

            def pair_of_chunks(n, carry):
                chunks = [
                    whole[UP, k, lax.div(n, 4), lax.rem(n, 4), c].astype(jnp.float32) for c in range(2)
                ]
                at = pl.ds(pl.multiple_of(48 * n, 16), 48)
                for half in range(2):
                    both = jnp.concatenate(side(chunks[0], half) + side(chunks[1], half), axis=0)
                    out_up[at, pl.ds(WIDE * k + HALF * half, HALF)] = both.astype(jnp.bfloat16)
                return carry

            lax.fori_loop(0, 16, pair_of_chunks, 0)
            return
        for half in range(2):
            chunks = whole[part, k].astype(jnp.float32)
            tile = jnp.concatenate(side(chunks, half), axis=-2)
            (out_down, out_mixed)[part - 1][pl.ds(WIDE * k + HALF * half, HALF), :] = (
                tile.reshape(768, HALF).T.astype(jnp.bfloat16)
            )

    def keep(part, k, rows, new, state):
        if part != MIXED:
            (new_up, new_down)[part][rows, columns[k]] = new
            (state_up, state_down)[part][rows, columns[k]] = state
            return
        mixed_own[0, rows, columns[k]] = new
        mixed_own[1, rows, columns[k]] = state
        gathered["kept"] = gathered.get("kept", 0) + 1
        if gathered["kept"] == sum(piece[0] == MIXED for piece in STREAMS):
            for row, targets in enumerate(
                ((new_query, new_key, new_value, new_mixed), (state_query, state_key, state_value, state_mixed))
            ):
                everything = mixed_own[row]
                for head in range(4):
                    targets[head][...] = everything[:, 192 * head : 192 * head + 192]

    def stream(part, k, first, count, axes, scatter_modes, gather_modes, lands):
        rows = pl.ds(first, count)
        copied = pl.ds(2 * first, 2 * count)
        lines = Lines(place, axes)

        def block(*index):
            return sums.at[(part, k) + index + (rows, slice(None))]

        def copy_block(*index):
            return whole.at[(part, k) + index + (copied, slice(None))]

        make_ready(part, k)
        coded, *lands = lands
        yield from coded_stage(sender, lines, block, coded, lands[0])
        for stage in (1, 2):
            yield from scatter_stage(sender, lines, stage, scatter_modes[stage], block, lands[stage])
        hold(part)
        own = sums[part, k, z, y, xh, rows, :] * mean_rate
        new, state = updated(own, held[0, part, rows, columns[k]], held[1, part, rows, columns[k]])
        keep(part, k, rows, new, state)
        whole[part, k, z, y, xh, copied, :] = jnp.concatenate(
            [new[:, :HALF], new[:, HALF:]], axis=0
        ).astype(jnp.bfloat16)
        for stage in (2, 1, 0):
            yield from gather_stage(sender, lines, stage, gather_modes[stage], copy_block)
        finish(part, k, (first, count))

    def norm_stream():
        for name in ("norm", "weight_norm", "moment_norm"):
            loads[name].wait()
        norm_rows[...] = jnp.zeros_like(norm_rows)
        norm_rows[1:2, 0:24] = norm_held[0]
        norm_rows[2:3, 0:24] = norm_held[1]
        placed = pltpu.roll(norm_rows[...], 24 * place.data, 1)
        norm_pair[xh, 0] = norm_grad[...]
        norm_pair[xh, 1] = placed[1:2]
        norm_pair[xh, 2] = placed[2:3]
        copy = sender.start(norm_pair.at[xh], norm_pair.at[xh], "x", 2)
        yield
        copy.wait_recv()
        norm_ring[0, y] = norm_pair[0] + norm_pair[1]
        copies = [sender.start(norm_ring.at[0, y], norm_ring.at[0, y], "y", s) for s in (1, 2, 3)]
        yield
        for copy in copies:
            copy.wait_recv()
        norm_ring[1, z] = norm_ring[0, 0] + norm_ring[0, 1] + norm_ring[0, 2] + norm_ring[0, 3]
        copies = [sender.start(norm_ring.at[1, z], norm_ring.at[1, z], "z", s) for s in (1, 2, 3)]
        yield
        for copy in copies:
            copy.wait_recv()
        total = norm_ring[1, 0] + norm_ring[1, 1] + norm_ring[1, 2] + norm_ring[1, 3]
        new, state = updated(total[0] * mean_rate, total[1], total[2])
        norm_all[...] = new
        norm_rows[0:1] = new
        norm_rows[1:2] = state
        own = pltpu.roll(norm_rows[...], lax.rem(768 - 24 * place.data, 768), 1)
        new_norm[...] = own[0:1, 0:24]
        state_norm[...] = own[1:2, 0:24]

    streams = []
    for n, piece in enumerate(STREAMS):
        streams.append(stream(*piece, landings[4 * n : 4 * n + 4]))
    streams.append(norm_stream())
    for part in (UP, DOWN, MIXED):
        make_ready(part, 0)
    pl.semaphore_wait(barrier, 7)
    for n in ORDER:
        next(streams[n], None)
    sender.finish()


def landing_shapes():
    shapes = []
    for part, k, first, count, axes, scatter_modes, gather_modes in STREAMS:
        lines = Lines.__new__(Lines)
        lines.axes = axes
        first_shape = (4 if axes[0] == "x" else 6, 3, count, WIDE)
        shapes += [pltpu.VMEM(first_shape, jnp.float32)] * 2
        for stage in (1, 2):
            twice = axes[stage] != "x" and scatter_modes[stage] == "t"
            slots = 1 if axes[stage] == "x" else 6 if twice else 3
            shapes.append(pltpu.VMEM((slots,) + lines.span(stage, twice) + (count, WIDE), jnp.float32))
    return shapes


def split_kernel(up, down, mixed, norm_all, *rest):
    kept, (copy_up, copy_down, *heads, copy_norm), others, sems = rest[:14], rest[14:21], rest[21:35], rest[35]
    pairs = [(up, copy_up), (down, copy_down)]
    pairs += [(mixed.at[pl.ds(192 * n, 192), :], head) for n, head in enumerate(heads)]
    pairs += list(zip(kept, others))
    copies = [pltpu.make_async_copy(source, target, sems.at[n]) for n, (source, target) in enumerate(pairs)]
    for copy in copies:
        copy.start()
    copy_norm[...] = norm_all[0].astype(jnp.bfloat16)
    for copy in copies:
        copy.wait()


def on_device(
    grad_up, grad_down, grad_query, grad_key, grad_value, grad_mixed, grad_norm,
    weight_up, weight_down, weight_query, weight_key, weight_value, weight_mixed, weight_norm,
    moment_up, moment_down, moment_query, moment_key, moment_value, moment_mixed, moment_norm,
):
    f32, bf16 = jnp.float32, jnp.bfloat16
    anywhere = pl.BlockSpec(memory_space=pl.ANY)
    shape = jax.ShapeDtypeStruct
    operands = (
        grad_up[0].reshape(4, 4, 2, 24, 768), grad_down[0],
        grad_query[0].T, grad_key[0].T, grad_value[0].T, grad_mixed[0], grad_norm,
        weight_up, weight_down.T, weight_query, weight_key, weight_value, weight_mixed.T, weight_norm[None],
        moment_up, moment_down.T, moment_query, moment_key, moment_value, moment_mixed.T, moment_norm[None],
    )
    vmem = pl.BlockSpec(memory_space=pltpu.VMEM)
    kept_shapes = ((24, 768),) * 2 + ((24, 192),) * 4 + ((1, 24),)
    inner = (pltpu.VMEM((768, 768), bf16),) * 3 + (pltpu.VMEM((1, 768), f32),)
    inner += tuple(pltpu.VMEM(s, f32) for s in kept_shapes * 2)
    results = pl.pallas_call(
        exchange_kernel,
        name="exchange",
        out_shape=inner,
        in_specs=[anywhere] * 21,
        out_specs=[vmem] * 18,
        scratch_shapes=[
            pltpu.VMEM((3, BLOCKS) + FOLDED, f32),
            pltpu.VMEM((2, 768, 768), f32),
            pltpu.VMEM((2, 3, 24, 768), f32),
            pltpu.VMEM((2, 4, 24, 192), f32),
            pltpu.VMEM((3, BLOCKS, 4, 4, 2, 48, HALF), bf16),
            pltpu.VMEM((2, 24, 768), f32),
            pltpu.VMEM((1, 768), f32),
            pltpu.VMEM((2, 1, 24), f32),
            pltpu.VMEM((8, 768), f32),
            pltpu.VMEM((2, 3, 1, 768), f32),
            pltpu.VMEM((2, 4, 3, 1, 768), f32),
            pltpu.SemaphoreType.DMA((SENDS,)),
            pltpu.SemaphoreType.DMA((SENDS,)),
            pltpu.SemaphoreType.DMA((28,)),
        ]
        + landing_shapes(),
        compiler_params=pltpu.CompilerParams(
            collective_id=0, has_side_effects=True, vmem_limit_bytes=56 * 2**20
        ),
    )(*operands)
    outs = pl.pallas_call(
        split_kernel,
        name="split",
        out_shape=(shape((768, 768), bf16),) * 2
        + (shape((192, 768), bf16),) * 4
        + (shape((768,), bf16),)
        + tuple(shape(s, f32) for s in kept_shapes * 2),
        in_specs=[vmem] * 18,
        out_specs=[anywhere] * 6 + [vmem] + [anywhere] * 14,
        scratch_shapes=[pltpu.SemaphoreType.DMA((20,))],
        compiler_params=pltpu.CompilerParams(vmem_limit_bytes=8 * 2**20),
    )(*results)
    copy_up, copy_down, copy_query, copy_key, copy_value, copy_mixed, copy_norm = outs[:7]

    def as_given(seven):
        up, down, query, key, value, mixed, norm = seven
        return (up, down.T, query, key, value, mixed.T, norm[0])

    return (
        (copy_up, copy_down, copy_query.T, copy_key.T, copy_value.T, copy_mixed, copy_norm)
        + as_given(outs[7:14])
        + as_given(outs[14:])
    )


def solution(mesh):
    return jax.shard_map(
        on_device,
        mesh=mesh,
        in_specs=(
            P("data", None, "width"),
            P("data", "width", None),
            P("data", None, "width"),
            P("data", None, "width"),
            P("data", None, "width"),
            P("data", "width", None),
            P("data", None),
        )
        + (
            P("data", "width"),
            P("width", "data"),
            P("data", "width"),
            P("data", "width"),
            P("data", "width"),
            P("width", "data"),
            P("data"),
        )
        * 2,
        out_specs=(
            P(None, "width"),
            P("width", None),
            P(None, "width"),
            P(None, "width"),
            P(None, "width"),
            P("width", None),
            P(),
        )
        + (
            P("data", "width"),
            P("width", "data"),
            P("data", "width"),
            P("data", "width"),
            P("data", "width"),
            P("width", "data"),
            P("data"),
        )
        * 2,
        check_vma=False,
    )
```

time: 99.1 us -> 66.7 us (0.67)
  Pallas kernels: 97 us -> 65.9 us
  other arithmetic: 1.28 us -> 0 us
    pallas_call x2, Pallas kernels: 97 us -> 65.9 us  [the longest x1 63.2 us: on_device(): pl.pallas_call(exchange_kernel, name='exchange', out_shape=inner, in_spec...]
    pallas_call x1 -> x0, other arithmetic: 1.28 us -> none  [on_device(): pl.pallas_call(split_kernel, name='split', out_shape=copy_shapes + (shape...]
where the time goes in v2:
time: 66.7 us; the launch traced here: 66.6 us
  Pallas kernels  65.9 us (99%)
  between operations  0.67 us (1%)
    pallas_call x1, Pallas kernels, on_device(): pl.pallas_call(exchange_kernel, name='exchange', out_shape=inner, in_spec...  63.2 us
    pallas_call x1, Pallas kernels, on_device(): pl.pallas_call(split_kernel, name='split', out_shape=(shape((768, 768), b...  2.73 us

profile of v2, /device:TPU:0, one launch (start us, length us, event | category | flops | bytes accessed | tf_op | source)
XLA Modules:
  0.0 66.6 jit_solution(4161969083481859463)
XLA Ops:
  0.7 63.2 %exchange.1 = (bf16[768,768]{1,0:T(8,128)(2,1)S(1)}, bf16[768,768]{1,0:T(8,128)(2,1)S(1)}, bf16[768,768]{1,0:T(8,128)(2,1)S(1)}, f32[1,768]{1,0:T(1,128)S(1)}, f...) custom-call(f32[4,4,2,24,768]{4,3,2,1,0:T(8,128)} %bitcast.27, ...), custom_call_target="tpu_custom_call" | custom-call | tf_op jit(solution)/shard_map/exchange/pallas_call | solution.py:523
  63.9 2.7 %split.1 = (bf16[768,768]{1,0:T(8,128)(2,1)}, bf16[768,768]{1,0:T(8,128)(2,1)}, bf16[192,768]{1,0:T(8,128)(2,1)}, bf16[192,768]{1,0:T(8,128)(2,1)}, bf16[192,768...) custom-call(bf16[768,768]{1,0:T(8,128)(2,1)S(1)} %get-tuple-element., ...), custom_call_target="tpu_custom_call" | custom-call | tf_op jit(solution)/shard_map/split/pallas_call | solution.py:550

commit v3 on v2

--- a/solution.py
+++ b/solution.py
@@ -16,23 +16,26 @@
 FOLDED = (4, 4, 2, 24, WIDE)
 BLOCKS = 3
 RAW = 6.0
-SENDS = 196
 STREAMS = (
     (UP, 0, 0, 24, "xyz", "dtd", "ddd"),
-    (DOWN, 0, 0, 24, "zyx", "ttd", "tdd"),
-    (MIXED, 0, 0, 24, "yzx", "ttd", "tdd"),
+    (DOWN, 0, 0, 24, "yxz", "tdd", "tdd"),
+    (MIXED, 0, 0, 24, "zxy", "tdd", "tdd"),
     (UP, 1, 0, 24, "xzy", "dtd", "ddd"),
     (DOWN, 1, 0, 24, "zyx", "ttd", "tdd"),
-    (MIXED, 1, 0, 24, "yzx", "ttd", "tdd"),
-    (UP, 2, 0, 24, "xyz", "dtd", "ddd"),
-    (DOWN, 2, 0, 24, "zyx", "ttd", "tdd"),
-    (MIXED, 2, 0, 24, "yzx", "ttd", "tdd"),
+    (MIXED, 1, 0, 24, "yxz", "tdd", "tdd"),
+    (UP, 2, 0, 16, "yxz", "tdd", "tdd"),
+    (DOWN, 2, 0, 16, "zyx", "ttd", "tdd"),
+    (MIXED, 2, 0, 16, "yzx", "tdd", "tdd"),
+    (UP, 2, 16, 8, "zxy", "tdd", "tdd"),
+    (DOWN, 2, 16, 8, "zxy", "tdd", "tdd"),
+    (MIXED, 2, 16, 8, "xzy", "ddd", "ddd"),
 )
 ORDER = (
-    0, 1, 2, 3, 4, 5, 6, 7, 8, 9, 1, 2, 4, 5, 0, 7, 8, 1, 2, 4, 3, 5, 0, 7,
-    2, 8, 1, 3, 4, 5, 6, 9, 0, 2, 7, 8, 1, 4, 3, 5, 6, 2, 0, 8, 9, 7, 1, 4,
-    3, 5, 6, 2, 0, 9, 8, 7, 1, 4, 3, 5, 6, 8, 2, 7, 0, 1, 4, 3, 5, 2, 6, 8,
-    7, 1, 5, 0, 4, 2, 7, 6, 3, 1, 8, 4, 7, 5, 8, 6,
+    0, 1, 2, 3, 4, 5, 6, 7, 8, 9, 10, 11, 12, 1, 2, 5, 4, 0, 6, 7, 9, 8, 10, 1,
+    2, 3, 5, 4, 0, 11, 7, 12, 9, 10, 6, 3, 1, 8, 4, 11, 2, 0, 7, 3, 12, 5, 4, 1,
+    9, 11, 10, 8, 2, 7, 6, 0, 12, 3, 4, 9, 5, 1, 10, 8, 11, 2, 7, 6, 0, 3, 4, 9,
+    5, 10, 1, 11, 8, 6, 2, 7, 9, 0, 3, 5, 10, 4, 8, 1, 11, 2, 6, 7, 9, 10, 5, 4,
+    8, 0, 2, 1, 7, 6, 9, 10, 5, 4, 8, 3, 7, 6,
 )
 
 
@@ -62,27 +65,40 @@
 
 
 class Sender:
-    def __init__(self, place, send_sems, recv_sems):
+    def __init__(self, place, send_sems, recv_sems, first):
         self.place, self.send_sems, self.recv_sems = place, send_sems, recv_sems
-        self.copies = []
-
-    def start(self, source, target, axis, step):
-        n = len(self.copies)
-        copy = pltpu.make_async_remote_copy(
+        self.next_send, self.next_recv = first
+        self.sent = []
+        self.turn = 0
+
+    def landing(self):
+        self.next_recv += 1
+        return self.recv_sems.at[self.next_recv - 1]
+
+    def begin(self, size):
+        sem = self.send_sems.at[self.next_send + self.turn]
+        self.turn = 1 - self.turn
+        if len(self.sent) == 2:
+            wait_for(*self.sent.pop(0))
+        self.sent.append((size, sem))
+
+    def start(self, source, target, axis, step, landing):
+        pltpu.make_async_remote_copy(
             src_ref=source,
             dst_ref=target,
-            send_sem=self.send_sems.at[n],
-            recv_sem=self.recv_sems.at[n],
+            send_sem=self.sent[-1][1],
+            recv_sem=landing,
             device_id=self.place.along(axis, step),
             device_id_type=MESH,
-        )
-        copy.start()
-        self.copies.append(copy)
-        return copy
+        ).start()
 
     def finish(self):
-        for copy in self.copies:
-            copy.wait_send()
+        for size, sem in self.sent:
+            wait_for(size, sem)
+
+
+def wait_for(size, sem):
+    pltpu.make_async_copy(size, size, sem).wait()
 
 
 def add_to(ref, *others):
@@ -154,9 +170,11 @@
         own = block(*lines.chosen(0, at))
         for n in range(4):
             coded[n] = encode(far[n], RAW)
-        copy = sender.start(coded, landing, axis, 2)
+        arrived = sender.landing()
+        sender.begin(landing)
+        sender.start(coded, landing, axis, 2, arrived)
         yield
-        copy.wait_recv()
+        wait_for(landing, arrived)
         for n in range(4):
             own[n] = own[n] + decode(landing[n], RAW)
         return
@@ -165,28 +183,27 @@
     def part(q, half):
         return block(*lines.chosen(0, q, half))
 
-    def send(n, values, largest, step):
+    far, final = sender.landing(), sender.landing()
+
+    def send(n, values, largest, step, arrived):
         coded[n] = encode(values, largest)
-        return sender.start(coded.at[n], landing.at[n], axis, step)
-
-    far_plus = send(0, fours(part(opposite, 0)), RAW, 1)
-    far_minus = send(1, fours(part(opposite, 1)), RAW, 3)
-    near_plus = send(2, fours(part(plus, 1)), RAW, 1)
-    near_minus = send(3, fours(part(minus, 0)), RAW, 3)
+        sender.start(coded.at[n], landing.at[n], axis, step, arrived)
+
+    sender.begin(landing.at[0:4])
+    send(0, fours(part(opposite, 0)), RAW, 1, far)
+    send(1, fours(part(opposite, 1)), RAW, 3, far)
+    send(2, fours(part(plus, 1)), RAW, 1, final)
+    send(3, fours(part(minus, 0)), RAW, 3, final)
     yield
-    far_plus.wait_recv()
-    both_plus = send(4, fours(part(plus, 0)) + decode(landing[0], RAW), 2 * RAW, 1)
-    far_minus.wait_recv()
-    both_minus = send(5, fours(part(minus, 1)) + decode(landing[1], RAW), 2 * RAW, 3)
+    wait_for(landing.at[0:2], far)
+    sender.begin(landing.at[4:6])
+    send(4, fours(part(plus, 0)) + decode(landing[0], RAW), 2 * RAW, 1, final)
+    send(5, fours(part(minus, 1)) + decode(landing[1], RAW), 2 * RAW, 3, final)
     yield
-    for near, near_slot, both, both_slot, half in (
-        (near_minus, 3, both_plus, 4, 0),
-        (near_plus, 2, both_minus, 5, 1),
-    ):
-        near.wait_recv()
-        both.wait_recv()
+    wait_for(landing.at[2:6], final)
+    for near, both, half in ((3, 4, 0), (2, 5, 1)):
         own = part(at, half)
-        total = fours(own) + decode(landing[near_slot], RAW) + decode(landing[both_slot], 2 * RAW)
+        total = fours(own) + decode(landing[near], RAW) + decode(landing[both], 2 * RAW)
         own[...] = total.reshape(own.shape)
 
 
@@ -194,44 +211,37 @@
     axis = lines.axes[stage]
     at = lines.at[axis]
     own = block(*lines.chosen(stage, at))
-    if axis == "x":
-        copy = sender.start(block(*lines.chosen(stage, 1 - at)), landing.at[0], axis, 2)
+    plus, minus, opposite = on_ring(at + 1), on_ring(at + 3), on_ring(at + 2)
+    if axis == "x" or mode == "d":
+        arrived = sender.landing()
+        sender.begin(landing)
+        targets = ((1 - at, 2),) if axis == "x" else ((opposite, 2), (plus, 1), (minus, 3))
+        for n, (q, step) in enumerate(targets):
+            sender.start(block(*lines.chosen(stage, q)), landing.at[n], axis, step, arrived)
         yield
-        copy.wait_recv()
-        add_to(own, landing.at[0])
-        return
-    plus, minus, opposite = on_ring(at + 1), on_ring(at + 3), on_ring(at + 2)
-    if mode == "d":
-        copies = [
-            sender.start(block(*lines.chosen(stage, q)), landing.at[n], axis, step)
-            for n, (q, step) in enumerate(((opposite, 2), (plus, 1), (minus, 3)))
-        ]
-        yield
-        for copy in copies:
-            copy.wait_recv()
-        add_to(own, *(landing.at[n] for n in range(3)))
+        wait_for(landing, arrived)
+        add_to(own, *(landing.at[n] for n in range(len(targets))))
         return
 
     def part(q, half):
         return block(*lines.chosen(stage, q, half))
 
-    far_plus = sender.start(part(opposite, 0), landing.at[0], axis, 1)
-    far_minus = sender.start(part(opposite, 1), landing.at[1], axis, 3)
-    near_plus = sender.start(part(plus, 1), landing.at[2], axis, 1)
-    near_minus = sender.start(part(minus, 0), landing.at[3], axis, 3)
+    far, final = sender.landing(), sender.landing()
+    sender.begin(landing.at[0:4])
+    sender.start(part(opposite, 0), landing.at[0], axis, 1, far)
+    sender.start(part(opposite, 1), landing.at[1], axis, 3, far)
+    sender.start(part(plus, 1), landing.at[2], axis, 1, final)
+    sender.start(part(minus, 0), landing.at[3], axis, 3, final)
     yield
-    far_plus.wait_recv()
+    wait_for(landing.at[0:2], far)
+    sender.begin(landing.at[4:6])
     add_to(part(plus, 0), landing.at[0])
-    both_plus = sender.start(part(plus, 0), landing.at[4], axis, 1)
-    far_minus.wait_recv()
+    sender.start(part(plus, 0), landing.at[4], axis, 1, final)
     add_to(part(minus, 1), landing.at[1])
-    both_minus = sender.start(part(minus, 1), landing.at[5], axis, 3)
+    sender.start(part(minus, 1), landing.at[5], axis, 3, final)
     yield
-    near_minus.wait_recv()
-    both_plus.wait_recv()
+    wait_for(landing.at[2:6], final)
     add_to(part(at, 0), landing.at[3], landing.at[4])
-    near_plus.wait_recv()
-    both_minus.wait_recv()
     add_to(part(at, 1), landing.at[2], landing.at[5])
 
 
@@ -240,28 +250,34 @@
     at = lines.at[axis]
     own = block(*lines.chosen(stage, at))
     if axis == "x" or mode == "d":
-        copies = [sender.start(own, own, axis, step) for step in ((2,) if axis == "x" else (2, 1, 3))]
+        steps = (2,) if axis == "x" else (2, 1, 3)
+        arrived = sender.landing()
+        size = block(*lines.chosen(stage, pl.ds(0, len(steps))))
+        sender.begin(size)
+        for step in steps:
+            sender.start(own, own, axis, step, arrived)
         yield
-        for copy in copies:
-            copy.wait_recv()
+        wait_for(size, arrived)
         return
 
     def part(q, half):
         return block(*lines.chosen(stage, q, half))
 
     plus, minus = on_ring(at + 1), on_ring(at + 3)
-    first_plus = sender.start(part(at, 0), part(at, 0), axis, 1)
-    first_minus = sender.start(part(at, 1), part(at, 1), axis, 3)
-    second_plus = sender.start(part(at, 1), part(at, 1), axis, 1)
-    second_minus = sender.start(part(at, 0), part(at, 0), axis, 3)
+    near, final = sender.landing(), sender.landing()
+    two = block(*lines.chosen(stage, pl.ds(0, 2)))
+    sender.begin(two)
+    sender.start(part(at, 0), part(at, 0), axis, 1, near)
+    sender.start(part(at, 1), part(at, 1), axis, 3, near)
+    sender.start(part(at, 1), part(at, 1), axis, 1, final)
+    sender.start(part(at, 0), part(at, 0), axis, 3, final)
     yield
-    first_plus.wait_recv()
-    on_plus = sender.start(part(minus, 0), part(minus, 0), axis, 1)
-    first_minus.wait_recv()
-    on_minus = sender.start(part(plus, 1), part(plus, 1), axis, 3)
+    wait_for(own, near)
+    sender.begin(own)
+    sender.start(part(minus, 0), part(minus, 0), axis, 1, final)
+    sender.start(part(plus, 1), part(plus, 1), axis, 3, final)
     yield
-    for copy in (second_plus, second_minus, on_plus, on_minus):
-        copy.wait_recv()
+    wait_for(two, final)
 
 
 def updated(mean, weight, moment):
@@ -293,30 +309,36 @@
 
     loads = {}
 
-    def load(name, source, target):
-        copy = pltpu.make_async_copy(source, target, load_sems.at[len(loads)])
-        copy.start()
-        loads[name] = copy
+    def load(name, *pairs, size=None):
+        sem = load_sems.at[len(loads)]
+        for source, target in pairs:
+            pltpu.make_async_copy(source, target, sem).start()
+        loads[name] = pairs[0][1] if size is None else size, sem
+
+    def loaded(name):
+        wait_for(*loads[name])
 
     heads = (grad_query, grad_key, grad_value, grad_mixed)
     for k in range(BLOCKS):
-        load((UP, k), grad_up.at[:, :, :, :, columns[k]], sums.at[UP, k])
-        load((DOWN, k), grad_down.at[columns[k], :], turned.at[0, columns[k], :])
+        load((UP, k), (grad_up.at[:, :, :, :, columns[k]], sums.at[UP, k]))
+        load((DOWN, k), (grad_down.at[columns[k], :], turned.at[0, columns[k], :]))
         for head in ((0, 1), (2,), (3,))[k]:
-            load(("head", head), heads[head], turned.at[1, pl.ds(192 * head, 192), :])
-    load("norm", grad_norm, norm_grad)
-    load("weight_norm", weight_norm, norm_held.at[0])
-    load("moment_norm", moment_norm, norm_held.at[1])
-    load(("weight", UP), weight_up, held.at[0, UP])
-    load(("moment", UP), moment_up, held.at[1, UP])
-    load(("weight", DOWN), weight_down, held.at[0, DOWN])
-    load(("moment", DOWN), moment_down, held.at[1, DOWN])
-    for head, source in enumerate((weight_query, weight_key, weight_value, weight_mixed)):
-        load(("weight head", head), source, held_heads.at[0, head])
-    for head, source in enumerate((moment_query, moment_key, moment_value, moment_mixed)):
-        load(("moment head", head), source, held_heads.at[1, head])
-
-    sender = Sender(place, send_sems, recv_sems)
+            load(("head", head), (heads[head], turned.at[1, pl.ds(192 * head, 192), :]))
+    load("norm", (grad_norm, norm_grad))
+    load("held norm", (weight_norm, norm_held.at[0]), (moment_norm, norm_held.at[1]), size=norm_held)
+    for part, weight, moment in ((UP, weight_up, moment_up), (DOWN, weight_down, moment_down)):
+        load(
+            ("held", part), (weight, held.at[0, part]), (moment, held.at[1, part]), size=held.at[:, part]
+        )
+    four_weights = (weight_query, weight_key, weight_value, weight_mixed)
+    four_moments = (moment_query, moment_key, moment_value, moment_mixed)
+    load(
+        ("held", MIXED),
+        *((source, held_heads.at[0, head]) for head, source in enumerate(four_weights)),
+        *((source, held_heads.at[1, head]) for head, source in enumerate(four_moments)),
+        size=held_heads,
+    )
+
     gathered = {}
     ready = set()
 
@@ -325,13 +347,13 @@
             return
         ready.add((part, k))
         if part == UP:
-            loads[UP, k].wait()
+            loaded((UP, k))
             return
         if part == DOWN:
-            loads[DOWN, k].wait()
+            loaded((DOWN, k))
         else:
             for head in ((0, 1), (2,), (3,))[k]:
-                loads["head", head].wait()
+                loaded(("head", head))
 
         def turn(n, carry):
             lanes = pl.ds(pl.multiple_of(384 * n, HALF), 384)
@@ -345,14 +367,10 @@
         if ("held", part) in ready:
             return
         ready.add(("held", part))
-        if part != MIXED:
-            loads["weight", part].wait()
-            loads["moment", part].wait()
-            return
-        for row, name in enumerate(("weight head", "moment head")):
-            for head in range(4):
-                loads[name, head].wait()
-            held[row, part] = jnp.concatenate([held_heads[row, head] for head in range(4)], axis=1)
+        loaded(("held", part))
+        if part == MIXED:
+            for row in range(2):
+                held[row, part] = jnp.concatenate([held_heads[row, head] for head in range(4)], axis=1)
 
     def finish(part, k, rows):
         done = gathered.setdefault((part, k), [])
@@ -404,7 +422,7 @@
                 for head in range(4):
                     targets[head][...] = everything[:, 192 * head : 192 * head + 192]
 
-    def stream(part, k, first, count, axes, scatter_modes, gather_modes, lands):
+    def stream(sender, part, k, first, count, axes, scatter_modes, gather_modes, lands):
         rows = pl.ds(first, count)
         copied = pl.ds(2 * first, 2 * count)
         lines = Lines(place, axes)
@@ -431,9 +449,9 @@
             yield from gather_stage(sender, lines, stage, gather_modes[stage], copy_block)
         finish(part, k, (first, count))
 
-    def norm_stream():
-        for name in ("norm", "weight_norm", "moment_norm"):
-            loads[name].wait()
+    def norm_stream(sender):
+        loaded("norm")
+        loaded("held norm")
         norm_rows[...] = jnp.zeros_like(norm_rows)
         norm_rows[1:2, 0:24] = norm_held[0]
         norm_rows[2:3, 0:24] = norm_held[1]
@@ -441,19 +459,20 @@
         norm_pair[xh, 0] = norm_grad[...]
         norm_pair[xh, 1] = placed[1:2]
         norm_pair[xh, 2] = placed[2:3]
-        copy = sender.start(norm_pair.at[xh], norm_pair.at[xh], "x", 2)
-        yield
-        copy.wait_recv()
+
+        def share(mine, axis, size):
+            arrived = sender.landing()
+            sender.begin(size)
+            for step in (2,) if axis == "x" else (1, 2, 3):
+                sender.start(mine, mine, axis, step, arrived)
+            yield
+            wait_for(size, arrived)
+
+        yield from share(norm_pair.at[xh], "x", norm_pair.at[0])
         norm_ring[0, y] = norm_pair[0] + norm_pair[1]
-        copies = [sender.start(norm_ring.at[0, y], norm_ring.at[0, y], "y", s) for s in (1, 2, 3)]
-        yield
-        for copy in copies:
-            copy.wait_recv()
+        yield from share(norm_ring.at[0, y], "y", norm_ring.at[0, 0:3])
         norm_ring[1, z] = norm_ring[0, 0] + norm_ring[0, 1] + norm_ring[0, 2] + norm_ring[0, 3]
-        copies = [sender.start(norm_ring.at[1, z], norm_ring.at[1, z], "z", s) for s in (1, 2, 3)]
-        yield
-        for copy in copies:
-            copy.wait_recv()
+        yield from share(norm_ring.at[1, z], "z", norm_ring.at[1, 0:3])
         total = norm_ring[1, 0] + norm_ring[1, 1] + norm_ring[1, 2] + norm_ring[1, 3]
         new, state = updated(total[0] * mean_rate, total[1], total[2])
         norm_all[...] = new
@@ -463,21 +482,30 @@
         new_norm[...] = own[0:1, 0:24]
         state_norm[...] = own[1:2, 0:24]
 
-    streams = []
-    for n, piece in enumerate(STREAMS):
-        streams.append(stream(*piece, landings[4 * n : 4 * n + 4]))
-    streams.append(norm_stream())
-    for part in (UP, DOWN, MIXED):
-        make_ready(part, 0)
+    senders, streams = [], []
+    first = 0
+    for n, piece in enumerate(STREAMS + (None,)):
+        senders.append(Sender(place, send_sems, recv_sems, (2 * n, first)))
+        if piece is None:
+            streams.append(norm_stream(senders[n]))
+        else:
+            streams.append(stream(senders[n], *piece, landings[4 * n : 4 * n + 4]))
+            first += waits_of(*piece[4:])
+    make_ready(UP, 0)
     pl.semaphore_wait(barrier, 7)
     for n in ORDER:
         next(streams[n], None)
-    sender.finish()
+    for sender in senders:
+        sender.finish()
+
+
+def waits_of(axes, scatter_modes, gather_modes):
+    return 6 + (scatter_modes + gather_modes).count("t")
 
 
 def landing_shapes():
     shapes = []
-    for part, k, first, count, axes, scatter_modes, gather_modes in STREAMS:
+    for _, _, _, count, axes, scatter_modes, _ in STREAMS:
         lines = Lines.__new__(Lines)
         lines.axes = axes
         first_shape = (4 if axes[0] == "x" else 6, 3, count, WIDE)
@@ -538,9 +566,9 @@
             pltpu.VMEM((8, 768), f32),
             pltpu.VMEM((2, 3, 1, 768), f32),
             pltpu.VMEM((2, 4, 3, 1, 768), f32),
-            pltpu.SemaphoreType.DMA((SENDS,)),
-            pltpu.SemaphoreType.DMA((SENDS,)),
-            pltpu.SemaphoreType.DMA((28,)),
+            pltpu.SemaphoreType.DMA((2 * len(STREAMS) + 2,)),
+            pltpu.SemaphoreType.DMA((sum(waits_of(*piece[4:]) for piece in STREAMS) + 3,)),
+            pltpu.SemaphoreType.DMA((15,)),
         ]
         + landing_shapes(),
         compiler_params=pltpu.CompilerParams(

time: 66.7 us -> 60.8 us (0.912)
  Pallas kernels: 65.9 us -> 60 us
    pallas_call x1, Pallas kernels: 63.2 us -> 57.3 us  [on_device(): pl.pallas_call(exchange_kernel, name='exchange', out_shape=inner, in_spec...]
where the time goes in v3:
time: 60.8 us; the launch traced here: 60.7 us
  Pallas kernels  60 us (99%)
  between operations  0.67 us (1%)
    pallas_call x1, Pallas kernels, on_device(): pl.pallas_call(exchange_kernel, name='exchange', out_shape=inner, in_spec...  57.3 us
    pallas_call x1, Pallas kernels, on_device(): pl.pallas_call(split_kernel, name='split', out_shape=(shape((768, 768), b...  2.73 us

profile of v3, /device:TPU:0, one launch (start us, length us, event | category | flops | bytes accessed | tf_op | source)
XLA Modules:
  0.0 60.7 jit_solution(5163621829519234968)
XLA Ops:
  0.7 57.3 %exchange.1 = (bf16[768,768]{1,0:T(8,128)(2,1)S(1)}, bf16[768,768]{1,0:T(8,128)(2,1)S(1)}, bf16[768,768]{1,0:T(8,128)(2,1)S(1)}, f32[1,768]{1,0:T(1,128)S(1)}, f...) custom-call(f32[4,4,2,24,768]{4,3,2,1,0:T(8,128)} %bitcast.27, ...), custom_call_target="tpu_custom_call" | custom-call | tf_op jit(solution)/shard_map/exchange/pallas_call | solution.py:551
  58.0 2.7 %split.1 = (bf16[768,768]{1,0:T(8,128)(2,1)}, bf16[768,768]{1,0:T(8,128)(2,1)}, bf16[192,768]{1,0:T(8,128)(2,1)}, bf16[192,768]{1,0:T(8,128)(2,1)}, bf16[192,768...) custom-call(bf16[768,768]{1,0:T(8,128)(2,1)S(1)} %get-tuple-element., ...), custom_call_target="tpu_custom_call" | custom-call | tf_op jit(solution)/shard_map/split/pallas_call | solution.py:578

commit v4 on v3

--- a/solution.py
+++ b/solution.py
@@ -17,25 +17,21 @@
 BLOCKS = 3
 RAW = 6.0
 STREAMS = (
-    (UP, 0, 0, 24, "xyz", "dtd", "ddd"),
-    (DOWN, 0, 0, 24, "yxz", "tdd", "tdd"),
-    (MIXED, 0, 0, 24, "zxy", "tdd", "tdd"),
-    (UP, 1, 0, 24, "xzy", "dtd", "ddd"),
-    (DOWN, 1, 0, 24, "zyx", "ttd", "tdd"),
-    (MIXED, 1, 0, 24, "yxz", "tdd", "tdd"),
-    (UP, 2, 0, 16, "yxz", "tdd", "tdd"),
-    (DOWN, 2, 0, 16, "zyx", "ttd", "tdd"),
-    (MIXED, 2, 0, 16, "yzx", "tdd", "tdd"),
-    (UP, 2, 16, 8, "zxy", "tdd", "tdd"),
-    (DOWN, 2, 16, 8, "zxy", "tdd", "tdd"),
-    (MIXED, 2, 16, 8, "xzy", "ddd", "ddd"),
+    (UP, 0, 0, 24, "zxy", "tdd", "tdd"),
+    (DOWN, 0, 0, 24, "xyz", "dtd", "ddd"),
+    (MIXED, 0, 0, 24, "xyz", "dtd", "ddd"),
+    (UP, 1, 0, 24, "yxz", "tdd", "tdd"),
+    (DOWN, 1, 0, 24, "yzx", "ttd", "tdd"),
+    (MIXED, 1, 0, 24, "zyx", "tdd", "tdd"),
+    (UP, 2, 0, 24, "zxy", "tdd", "tdd"),
+    (DOWN, 2, 0, 24, "yzx", "tdd", "tdd"),
+    (MIXED, 2, 0, 24, "zxy", "tdd", "tdd"),
 )
 ORDER = (
-    0, 1, 2, 3, 4, 5, 6, 7, 8, 9, 10, 11, 12, 1, 2, 5, 4, 0, 6, 7, 9, 8, 10, 1,
-    2, 3, 5, 4, 0, 11, 7, 12, 9, 10, 6, 3, 1, 8, 4, 11, 2, 0, 7, 3, 12, 5, 4, 1,
-    9, 11, 10, 8, 2, 7, 6, 0, 12, 3, 4, 9, 5, 1, 10, 8, 11, 2, 7, 6, 0, 3, 4, 9,
-    5, 10, 1, 11, 8, 6, 2, 7, 9, 0, 3, 5, 10, 4, 8, 1, 11, 2, 6, 7, 9, 10, 5, 4,
-    8, 0, 2, 1, 7, 6, 9, 10, 5, 4, 8, 3, 7, 6,
+    0, 3, 6, 1, 2, 4, 5, 7, 8, 9, 0, 3, 6, 4, 1, 5, 7, 8, 3, 4, 2, 0, 9, 1,
+    6, 7, 5, 3, 8, 2, 4, 9, 0, 1, 7, 6, 5, 3, 4, 2, 9, 8, 0, 1, 7, 6, 5, 3,
+    4, 2, 8, 0, 1, 7, 6, 5, 3, 4, 2, 8, 0, 7, 1, 6, 5, 4, 3, 8, 0, 2, 6, 7,
+    5, 1, 4, 8, 3, 7, 0, 6, 2, 4, 5, 8,
 )
 
 
@@ -141,6 +137,57 @@
 
 
 def encode(values, largest):
+    if values.shape[-2] == 24:
+        return three_as_two(values[:, 0:8], values[:, 8:16], values[:, 16:24], largest)
+    return four_as_three(values, largest)
+
+
+def decode(coded, largest):
+    if coded.shape[0] == 4:
+        return three_of_two(coded[:, 0:8], coded[:, 8:16], largest)
+    return four_of_three(coded, largest)
+
+
+def three_as_two(one, two, third, largest):
+    steps = jnp.floor(third * (127000 / largest) + 127008.5)
+    high = jnp.floor((steps + 0.5) * (1 / 504))
+    both = []
+    for value, digit in ((one, high), (two, steps - high * 504.0)):
+        level = jnp.floor((digit + 0.5) * (1 / 63))
+        beside = digit - level * 63.0 + 1.0
+        top = level >= 4.0
+        rest = jnp.where(top, level - 4.0, level)
+        middle = rest >= 2.0
+        rest = jnp.where(middle, rest - 2.0, rest)
+        power = jnp.where(top, 2.0**-25, 2.0**-125)
+        power = jnp.where(middle, power * 2.0**50, power)
+        power = jnp.where(rest >= 1.0, power * 2.0**25, power)
+        whole = jnp.floor(value * ((2**18 - 1) / largest) + 0.5) * 64.0
+        both.append((whole + beside) * power)
+    return jnp.concatenate(both, axis=1)
+
+
+def three_of_two(one, two, largest):
+    values, digits = [], []
+    for coded in (one, two):
+        size = jnp.abs(coded)
+        top = size >= 2.0**-25
+        power = jnp.where(top, 2.0**25, 2.0**125)
+        size = size * power
+        middle = size >= 2.0**50
+        down = jnp.where(middle, 2.0**-50, 1.0)
+        size, power = size * down, power * down
+        low = size >= 2.0**25
+        whole = coded * jnp.where(low, power * 2.0**-25, power)
+        level = jnp.where(top, 4.0, 0.0) + jnp.where(middle, 2.0, 0.0) + jnp.where(low, 1.0, 0.0)
+        value = jnp.floor(whole * 2.0**-6)
+        digits.append(level * 63.0 + (whole - value * 64.0 - 1.0))
+        values.append(value * (largest / (2**18 - 1)))
+    third = (digits[0] * 504.0 + digits[1] - 127008.0) * (largest / 127000)
+    return jnp.concatenate(values + [third], axis=1)
+
+
+def four_as_three(values, largest):
     first = jnp.floor(values[:3] * ((2**18 - 1) / largest) + 0.5) * 64.0
     fourth = jnp.floor(values[3] * ((2**17 - 1) / largest) + (2**17 + 0.5))
     high = jnp.floor(fourth * 2.0**-12)
@@ -149,7 +196,7 @@
     return first + jnp.stack([high, middle, rest - middle * 64.0])
 
 
-def decode(coded, largest):
+def four_of_three(coded, largest):
     first = jnp.floor(coded * 2.0**-6)
     digits = coded - first * 64.0
     fourth = (digits[0] * 64.0 + digits[1]) * 64.0 + (digits[2] - 2.0**17)
@@ -508,7 +555,8 @@
     for _, _, _, count, axes, scatter_modes, _ in STREAMS:
         lines = Lines.__new__(Lines)
         lines.axes = axes
-        first_shape = (4 if axes[0] == "x" else 6, 3, count, WIDE)
+        coded_shape = (4, 16, WIDE) if count == 24 else (3, count, WIDE)
+        first_shape = (4 if axes[0] == "x" else 6,) + coded_shape
         shapes += [pltpu.VMEM(first_shape, jnp.float32)] * 2
         for stage in (1, 2):
             twice = axes[stage] != "x" and scatter_modes[stage] == "t"

time: 60.8 us -> 59 us (0.970)
  Pallas kernels: 60 us -> 58.2 us
    pallas_call x1, Pallas kernels: 57.3 us -> 55.5 us  [on_device(): pl.pallas_call(exchange_kernel, name='exchange', out_shape=inner, in_spec...]
where the time goes in v4:
time: 59 us; the launch traced here: 58.9 us
  Pallas kernels  58.2 us (99%)
  between operations  0.67 us (1%)
    pallas_call x1, Pallas kernels, on_device(): pl.pallas_call(exchange_kernel, name='exchange', out_shape=inner, in_spec...  55.5 us
    pallas_call x1, Pallas kernels, on_device(): pl.pallas_call(split_kernel, name='split', out_shape=(shape((768, 768), b...  2.73 us

profile of v4, /device:TPU:0, one launch (start us, length us, event | category | flops | bytes accessed | tf_op | source)
XLA Modules:
  0.0 58.9 jit_solution(13269335601896261533)
XLA Ops:
  0.7 55.5 %exchange.1 = (bf16[768,768]{1,0:T(8,128)(2,1)S(1)}, bf16[768,768]{1,0:T(8,128)(2,1)S(1)}, bf16[768,768]{1,0:T(8,128)(2,1)S(1)}, f32[1,768]{1,0:T(1,128)S(1)}, f...) custom-call(f32[4,4,2,24,768]{4,3,2,1,0:T(8,128)} %bitcast.27, ...), custom_call_target="tpu_custom_call" | custom-call | tf_op jit(solution)/shard_map/exchange/pallas_call | solution.py:599
  56.2 2.7 %split.1 = (bf16[768,768]{1,0:T(8,128)(2,1)}, bf16[768,768]{1,0:T(8,128)(2,1)}, bf16[192,768]{1,0:T(8,128)(2,1)}, bf16[192,768]{1,0:T(8,128)(2,1)}, bf16[192,768...) custom-call(bf16[768,768]{1,0:T(8,128)(2,1)S(1)} %get-tuple-element., ...), custom_call_target="tpu_custom_call" | custom-call | tf_op jit(solution)/shard_map/split/pallas_call | solution.py:626

commit v5 on v4

--- a/solution.py
+++ b/solution.py
@@ -66,9 +66,19 @@
         self.next_send, self.next_recv = first
         self.sent = []
         self.turn = 0
+        self.taken, self.spare = {}, []
+
+    def scatters(self, stage):
+        self.spare, self.taken[stage] = [], []
+
+    def gathers(self, stage):
+        self.spare = list(self.taken.get(stage - 1, ()))
 
     def landing(self):
+        if self.spare:
+            return self.recv_sems.at[self.spare.pop()]
         self.next_recv += 1
+        self.taken[max(self.taken, default=0)] = self.taken.get(max(self.taken, default=0), []) + [self.next_recv - 1]
         return self.recv_sems.at[self.next_recv - 1]
 
     def begin(self, size):
@@ -482,8 +492,10 @@
 
         make_ready(part, k)
         coded, *lands = lands
+        sender.scatters(0)
         yield from coded_stage(sender, lines, block, coded, lands[0])
         for stage in (1, 2):
+            sender.scatters(stage)
             yield from scatter_stage(sender, lines, stage, scatter_modes[stage], block, lands[stage])
         hold(part)
         own = sums[part, k, z, y, xh, rows, :] * mean_rate
@@ -493,6 +505,7 @@
             [new[:, :HALF], new[:, HALF:]], axis=0
         ).astype(jnp.bfloat16)
         for stage in (2, 1, 0):
+            sender.gathers(stage)
             yield from gather_stage(sender, lines, stage, gather_modes[stage], copy_block)
         finish(part, k, (first, count))
 
@@ -547,7 +560,10 @@
 
 
 def waits_of(axes, scatter_modes, gather_modes):
-    return 6 + (scatter_modes + gather_modes).count("t")
+    scatters = [1 + (mode == "t") for mode in scatter_modes]
+    gathers = [1 + (mode == "t") for mode in gather_modes]
+    again = min(gathers[2], scatters[1]) + min(gathers[1], scatters[0])
+    return sum(scatters) + sum(gathers) - again
 
 
 def landing_shapes():

time: 59 us -> 58.8 us (level)
  no operation moved by 1% of the time
where the time goes in v5:
time: 58.8 us; the launch traced here: 58.7 us
  Pallas kernels  58.1 us (99%)
  between operations  0.67 us (1%)
    pallas_call x1, Pallas kernels, on_device(): pl.pallas_call(exchange_kernel, name='exchange', out_shape=inner, in_spec...  55.3 us
    pallas_call x1, Pallas kernels, on_device(): pl.pallas_call(split_kernel, name='split', out_shape=(shape((768, 768), b...  2.73 us

profile of v5, /device:TPU:0, one launch (start us, length us, event | category | flops | bytes accessed | tf_op | source)
XLA Modules:
  0.0 58.7 jit_solution(399472996260732085)
XLA Ops:
  0.7 55.3 %exchange.1 = (bf16[768,768]{1,0:T(8,128)(2,1)S(1)}, bf16[768,768]{1,0:T(8,128)(2,1)S(1)}, bf16[768,768]{1,0:T(8,128)(2,1)S(1)}, f32[1,768]{1,0:T(1,128)S(1)}, f...) custom-call(f32[4,4,2,24,768]{4,3,2,1,0:T(8,128)} %bitcast.27, ...), custom_call_target="tpu_custom_call" | custom-call | tf_op jit(solution)/shard_map/exchange/pallas_call | solution.py:615
  56.0 2.7 %split.1 = (bf16[768,768]{1,0:T(8,128)(2,1)}, bf16[768,768]{1,0:T(8,128)(2,1)}, bf16[192,768]{1,0:T(8,128)(2,1)}, bf16[192,768]{1,0:T(8,128)(2,1)}, bf16[192,768...) custom-call(bf16[768,768]{1,0:T(8,128)(2,1)S(1)} %get-tuple-element., ...), custom_call_target="tpu_custom_call" | custom-call | tf_op jit(solution)/shard_map/split/pallas_call | solution.py:642
